TPU v7x, 32 devices: a whole 2x2x4 slice. The times are simulated.
32 devices in a mesh: fov: 8 (over z, x), row: 4 (over y, core).
Axes of the slice: x: 2, y: 2, z: 4, core: 2. Of those that a mesh axis runs over, the one named last changes fastest.
Arguments:
- frames: bfloat16 [8, 5, 512, 512], P('fov', None, 'row'), parts along dimension 0, may hold values from 0.01 to 13, as said below
- phase_offset: float32 [8], P('fov'), parts along dimension 0, may hold values from -3.140625 to 3.140625
- order_gain: float32 [8, 5], P('fov'), parts along dimension 0, may hold values from 0.5 to 2
- band_shift: int32 [8, 2], P('fov'), parts along dimension 0, may hold values from -96 to 96
Outputs:
- picture: float32 [8192, 1024], P(('fov', 'row')), parts along dimension 0
There are 8 independent parts, one for each index of `fov`. A program takes and returns all parts, laid end to end along the dimension named above; each array names one. Nothing has to cross between parts.
Inputs may be any that keep to these rules, and one draw needn't show every extreme that they name: `frames`: positive intensities. `band_shift`: offsets in frequency bins of the 1024-point grid, row component first.
All inputs are finite; a program needn't handle non-finite values.
Results may differ from a plain program's by a relative error of at most 0.0003.
Values sent between devices are 32-bit elements; how exact they have to be, the bound alone decides.
A program may use at most 128 MiB of HBM per device.

v0:
```python
import functools
import math

import jax
import jax.numpy as jnp
import numpy as np
from jax import lax
from jax.experimental import pallas as pl
from jax.experimental.pallas import tpu as pltpu
from jax.sharding import PartitionSpec as P

MESH = pl.DeviceIdType.MESH
wiener = 0.1
gain_out = 8.0
cut_share = 0.45
CORES = 2


def split_table(table):
    high = table.astype(np.float32).astype(jnp.bfloat16)
    low = (table - high.astype(np.float64)).astype(np.float32).astype(jnp.bfloat16)
    return np.stack([high, low])


def cos_sin(points, freqs, length):
    angle = 2.0 * math.pi * ((points[:, None] * freqs[None, :]) % length) / length
    return np.cos(angle), np.sin(angle)


def tables(pixels, count):
    half = pixels // 2
    share = half // count
    chips = count // CORES
    points = np.arange(pixels)
    freqs = np.arange(half)
    alternate = 1.0 - 2.0 * (points % 2)
    cos_f, sin_f = cos_sin(points, freqs, pixels)
    sin_f[:, 0] = alternate

    def by_device(cos_part, sin_part):
        rows = cos_part.shape[0]
        both = np.stack([cos_part.reshape(rows, count, share), sin_part.reshape(rows, count, share)], axis=2)
        return both.reshape(rows, count * 2 * share)

    width = CORES * 2 * share
    lead = by_device(cos_f, sin_f).reshape(pixels, chips, width).transpose(1, 0, 2)
    column = np.concatenate([cos_f, sin_f], axis=1).T
    column = column.reshape(pixels, chips, pixels // chips).transpose(1, 0, 2)
    inverse = []
    for odd in range(2):
        cos_i, sin_i = cos_sin(2 * points + odd, freqs, 2 * pixels)
        sin_i[:, 0] = alternate
        inverse.append(np.concatenate([cos_i, sin_i], axis=1))
    inverse = np.stack(inverse)
    wide = np.arange(2 * pixels)
    cos_w, sin_w = cos_sin(wide, freqs, 2 * pixels)
    sin_w[:, 0] = 1.0 - 2.0 * ((wide // 2) % 2)
    last = by_device(cos_w, sin_w).T.reshape(chips, width, 2 * pixels)
    return tuple(split_table(t) for t in (lead, column, inverse, last))


def otf_polynomial():
    nodes = 0.5 + 0.5 * np.cos(math.pi * (np.arange(64) + 0.5) / 64)
    nodes = np.minimum(nodes, 0.9985)
    root = np.sqrt(1 - nodes * nodes)
    values = 2 / math.pi * (np.arccos(nodes) - nodes * root) / root**3
    fit = np.polynomial.chebyshev.Chebyshev.fit(nodes, values, 10, domain=[0, 1])
    poly = fit.convert(kind=np.polynomial.Polynomial).coef
    return [float(c) for c in poly[::-1]]


def halves(value):
    high = value.astype(jnp.bfloat16)
    return high, (value - high.astype(jnp.float32)).astype(jnp.bfloat16)


def dot(left, right):
    return jnp.dot(left, right, preferred_element_type=jnp.float32)


def dot3(left_hi, left_lo, right_hi, right_lo):
    return dot(left_hi, right_hi) + (dot(left_hi, right_lo) + dot(left_lo, right_hi))


def kernel(count, poly, frames, offset, gain, shift, lead_h, column_h, inverse_h, last_h, out,
           lead, column, inverse, last, tot_send, tot, planes, send1, recv1, mixed, weights, coef,
           send2, recv2, woven, table_sem, tot_ss, tot_rs, ss1, rs1, ss2, rs2):
    me = lax.axis_index("row")
    chips = count // CORES
    chip, core = me // CORES, me % CORES
    phases, rows, pixels = frames.shape[1:]
    half = pixels // 2
    share = half // count
    lanes = 2 * share
    others = [lax.rem(me + step, count) for step in range(1, count)]
    far_chips = [lax.rem(chip + step, chips) for step in range(1, chips)]
    sibling = chip * CORES + 1 - core
    far = [(c, c * CORES + k) for c in far_chips for k in range(CORES)]

    loads = []
    for idx, (source, target) in enumerate(
        ((lead_h, lead), (column_h, column), (inverse_h, inverse), (last_h, last))
    ):
        loads.append(pltpu.make_async_copy(source, target, table_sem.at[idx]))
    loads[0].start()

    lane8 = lax.broadcasted_iota(jnp.int32, (8, 128), 1)
    part = jnp.zeros((8, 128), jnp.float32)
    for p in range(phases):
        f = frames[0, p].astype(jnp.float32)
        s = jnp.sum(jnp.sum(f, axis=0, keepdims=True), axis=1, keepdims=True)
        part = part + jnp.where(lane8 == p, s, 0.0)
    tot_send[...] = part
    tot[me] = part

    barrier = pltpu.get_barrier_semaphore()
    for peer in others:
        pl.semaphore_signal(barrier, inc=1, device_id={"row": peer}, device_id_type=MESH)
    pl.semaphore_wait(barrier, count - 1)

    def tot_copy(peer, slot):
        return pltpu.make_async_remote_copy(
            src_ref=tot_send, dst_ref=tot.at[slot], send_sem=tot_ss.at[peer], recv_sem=tot_rs.at[slot],
            device_id={"row": peer}, device_id_type=MESH)

    for peer in others:
        tot_copy(peer, me).start()
    for load in loads[1:]:
        load.start()

    shift_y, shift_x = shift[0, 0], shift[0, 1]
    inv_cut = 1.0 / (cut_share * pixels)
    scale_out = gain_out / (4.0 * pixels * pixels)

    def wrap(value):
        return ((value + half) & (pixels - 1)) - half

    def lane_freq(shape):
        lane = lax.broadcasted_iota(jnp.int32, shape, 1)
        base = me * share
        plus = base + lane
        minus = base + lane - share
        minus = jnp.where(minus == 0, -half, minus)
        return jnp.where(lane < share, plus, -minus)

    def row_freq(first, sign, shape):
        row = first + lax.broadcasted_iota(jnp.int32, shape, 0)
        if sign == 0:
            return row
        return jnp.where(row == 0, half, -row)

    def placed(freq, order, shift_val):
        return order * shift_val + wrap(freq - order * shift_val)

    def curve(sq_y, sq_x):
        t = jnp.minimum(sq_y + sq_x, 1.0)
        r = t * lax.rsqrt(jnp.maximum(t, 1e-30))
        u = 1.0 - t
        v = u * lax.rsqrt(jnp.maximum(u, 1e-30))
        acc = jnp.full(t.shape, poly[0], jnp.float32)
        for c in poly[1:]:
            acc = acc * r + c
        return acc * (u * v)

    step = 16
    orders = phases // 2 + 1
    mid = phases // 2
    gains = [gain[0, j] for j in range(phases)]

    def make_weights(order):
        big_x = placed(lane_freq((step, lanes)), order, shift_x)
        sq_xs = []
        for j in range(phases):
            fx = (big_x - (j - mid) * shift_x).astype(jnp.float32) * inv_cut
            sq_xs.append(fx * fx)

        def body(i, carry):
            first = pl.multiple_of(i * step, step)
            for sign in range(2):
                big_y = placed(row_freq(first, sign, (step, lanes)), order, shift_y)
                den = jnp.full((step, lanes), wiener, jnp.float32)
                den_m = jnp.full((step, lanes), wiener, jnp.float32)
                own = None
                for j in range(phases):
                    fy = (big_y - (j - mid) * shift_y).astype(jnp.float32) * inv_cut
                    value = curve(fy * fy, sq_xs[j])
                    sq = value * value
                    den = den + (gains[j] * gains[j]) * sq
                    den_m = den_m + (gains[phases - 1 - j] * gains[phases - 1 - j]) * sq
                    if j == mid + order:
                        own = value
                if order == 0:
                    w = own * (gains[mid] * scale_out) / den
                else:
                    w = own * scale_out * (gains[mid + order] / den + gains[mid - order] / den_m)
                weights[order, sign, pl.ds(first, step), :] = w
            return carry

        lax.fori_loop(0, half // step, body, 0)

    col = lax.broadcasted_iota(jnp.int32, (8, pixels), 1)
    row = lax.broadcasted_iota(jnp.int32, (rows, 128), 0) + me * rows
    turn = 2.0 * math.pi / pixels
    waves = {}
    for order in range(1, orders):
        arg_x = ((col * (order * shift_x)) & (pixels - 1)).astype(jnp.float32) * turn
        arg_y = ((row * (order * shift_y)) & (pixels - 1)).astype(jnp.float32) * turn
        waves[order] = (jnp.cos(arg_x)[:1], jnp.sin(arg_x)[:1], jnp.cos(arg_y)[:, :1], jnp.sin(arg_y)[:, :1])
    angle = 2.0 * math.pi / phases * lane8.astype(jnp.float32) + offset[0]
    unmix = {order: (jnp.cos(order * angle), jnp.sin(order * angle)) for order in range(orders)}

    for peer in others:
        tot_copy(peer, peer).wait_recv()
    total = tot[0]
    for d in range(1, count):
        total = total + tot[d]
    level = jnp.where(lane8 < phases, float(pixels * pixels), 0.0) / jnp.where(lane8 < phases, total, 1.0)
    level = level / phases

    groups = [(0, 2), (2, 2), (4, 1)]

    def send1_copy(dest, slot_chip, slot_core, source, g):
        first, wide = groups[g]
        window = pl.ds(first * lanes, wide * lanes)
        return pltpu.make_async_remote_copy(
            src_ref=send1.at[dest, :, window],
            dst_ref=recv1.at[slot_chip, pl.ds(pl.multiple_of(slot_core * rows, rows), rows), window],
            send_sem=ss1.at[dest, g], recv_sem=rs1.at[source, g],
            device_id={"row": dest}, device_id_type=MESH)

    loads[0].wait()
    for g, (first, wide) in enumerate(groups):
        order = 0 if wide == 1 else g + 1
        coef_re = level * unmix[order][0]
        if order == 0:
            band = coef_re[:1, 0:1] * frames[0, 0].astype(jnp.float32)
            for p in range(1, phases):
                band = band + coef_re[:1, p:p + 1] * frames[0, p].astype(jnp.float32)
            parts = [band]
        else:
            coef_im = -level * unmix[order][1]
            band_re = coef_re[:1, 0:1] * frames[0, 0].astype(jnp.float32)
            band_im = coef_im[:1, 0:1] * frames[0, 0].astype(jnp.float32)
            for p in range(1, phases):
                f = frames[0, p].astype(jnp.float32)
                band_re = band_re + coef_re[:1, p:p + 1] * f
                band_im = band_im + coef_im[:1, p:p + 1] * f
            cx, sx, cy, sy = waves[order]
            ph_re = cy * cx - sy * sx
            ph_im = cy * sx + sy * cx
            parts = [band_re * ph_re - band_im * ph_im, band_re * ph_im + band_im * ph_re]
        for k, value in enumerate(parts):
            hi, lo = halves(value)
            planes[0, pl.ds((first + k) * rows, rows), :] = hi
            planes[1, pl.ds((first + k) * rows, rows), :] = lo
        span = pl.ds(first * rows, wide * rows)
        for c in far_chips:
            result = dot3(planes[0, span, :], planes[1, span, :], lead[0, c], lead[1, c])
            for k in range(wide):
                for kc in range(CORES):
                    send1[c * CORES + kc, :, pl.ds((first + k) * lanes, lanes)] = result[
                        k * rows:(k + 1) * rows, kc * lanes:(kc + 1) * lanes]
            for kc in range(CORES):
                send1_copy(c * CORES + kc, chip, core, me, g).start()
    mine = pl.ds(pl.multiple_of(core * rows, rows), rows)
    for g, (first, wide) in enumerate(groups):
        span = pl.ds(first * rows, wide * rows)
        result = dot3(planes[0, span, :], planes[1, span, :], lead[0, chip], lead[1, chip])
        for k in range(wide):
            block = result[k * rows:(k + 1) * rows]
            low_half, high_half = block[:, :lanes], block[:, lanes:]
            window = pl.ds((first + k) * lanes, lanes)
            recv1[chip, mine, window] = jnp.where(core == 0, low_half, high_half)
            send1[sibling, :, window] = jnp.where(core == 0, high_half, low_half)
        send1_copy(sibling, chip, core, me, g).start()

    for order in range(orders):
        make_weights(order)

    loads[1].wait()
    for g, (first, wide) in enumerate(groups):
        window = pl.ds(first * lanes, wide * lanes)
        send1_copy(sibling, chip, 1 - core, sibling, g).wait_recv()
        hi, lo = halves(recv1[chip, :, window])
        mixed[:, window] = dot3(column[0, chip], column[1, chip], hi, lo)
    for c in far_chips:
        for g, (first, wide) in enumerate(groups):
            window = pl.ds(first * lanes, wide * lanes)
            for kc in range(CORES):
                send1_copy(c * CORES + kc, c, kc, c * CORES + kc, g).wait_recv()
            hi, lo = halves(recv1[c, :, window])
            mixed[:, window] += dot3(column[0, c], column[1, c], hi, lo)

    lane = lax.broadcasted_iota(jnp.int32, (step, lanes), 1)
    low_lanes = lane < share
    special = jnp.logical_and(me == 0, jnp.logical_or(lane == 0, lane == share))
    special_top = jnp.logical_and(special, lane == share)
    freq_x = lane_freq((step, lanes))
    sign_x = jnp.where(low_lanes, 1.0, -1.0)
    parity_x = []
    for order in range(orders):
        turns = (placed(freq_x, order, shift_x) - freq_x) // pixels
        parity_x.append((1 - 2 * (turns & 1)).astype(jnp.float32))

    def turn_lanes(value):
        return pltpu.roll(value, share, 1)

    def combine(i, carry):
        first = pl.multiple_of(i * step, step)
        row0 = (first + lax.broadcasted_iota(jnp.int32, (step, lanes), 0)) == 0
        spectra = []
        for plane in range(phases):
            window = pl.ds(plane * lanes, lanes)
            upper = mixed[pl.ds(first, step), window]
            lower = mixed[pl.ds(half + first, step), window]
            upper_t, lower_t = turn_lanes(upper), turn_lanes(lower)
            as_is = jnp.logical_or(low_lanes, special)
            cc = jnp.where(as_is, upper, upper_t)
            sc = jnp.where(as_is, lower, lower_t)
            cs = jnp.where(special, 0.0, jnp.where(low_lanes, upper_t, upper)) * sign_x
            ss = jnp.where(special, 0.0, jnp.where(low_lanes, lower_t, lower)) * sign_x
            plus = (jnp.where(row0, cc, cc - ss), -jnp.where(row0, cs, sc + cs))
            minus = (jnp.where(row0, sc, cc + ss), jnp.where(row0, -ss, sc - cs))
            spectra.append((plus, minus))
        terms = []
        for sign in range(2):
            freq_y = row_freq(first, sign, (step, lanes))
            for order in range(orders):
                if order == 0:
                    re, im = spectra[phases - 1][sign]
                else:
                    rr, ri = spectra[2 * order - 2][sign]
                    ir, ii = spectra[2 * order - 1][sign]
                    re, im = rr - ii, ri + ir
                w = weights[order, sign, pl.ds(first, step), :]
                turns = (placed(freq_y, order, shift_y) - freq_y) // pixels
                terms.append((re * w, im * w, (1 - 2 * (turns & 1)).astype(jnp.float32)))
        for a in range(2):
            for b in range(2):
                sums = []
                for sign in range(2):
                    tot_re, tot_im = None, None
                    for order in range(orders):
                        re, im, par_y = terms[sign * orders + order]
                        factor = None
                        if a:
                            factor = par_y
                        if b:
                            factor = parity_x[order] if factor is None else factor * parity_x[order]
                        if factor is not None:
                            re, im = re * factor, im * factor
                        tot_re = re if tot_re is None else tot_re + re
                        tot_im = im if tot_im is None else tot_im + im
                    sums.append((tot_re, tot_im))
                (pr, pi), (mr, mi) = sums
                even_r = jnp.where(row0, pr, pr + mr)
                even_i = jnp.where(row0, pi, pi + mi)
                if a == 0:
                    odd_r = jnp.where(row0, mi, pr - mr)
                    odd_i = jnp.where(row0, -mr, pi - mi)
                else:
                    odd_r = jnp.where(row0, mr, pr - mr)
                    odd_i = jnp.where(row0, mi, pi - mi)

                def fold(x, y):
                    lo_val = x + turn_lanes(x)
                    hi_val = y - turn_lanes(y)
                    res = jnp.where(low_lanes, lo_val, hi_val)
                    res = jnp.where(special, x, res)
                    if b:
                        res = jnp.where(special_top, -y, res)
                    return res

                upper = fold(even_r, even_i)
                lower = fold(-odd_i, odd_r)
                window = pl.ds(b * lanes, lanes)
                hi, lo = halves(upper)
                coef[0, a, pl.ds(first, step), window] = hi
                coef[1, a, pl.ds(first, step), window] = lo
                hi, lo = halves(lower)
                coef[0, a, pl.ds(half + first, step), window] = hi
                coef[1, a, pl.ds(half + first, step), window] = lo
        return carry

    lax.fori_loop(0, half // step, combine, 0)

    def send2_copy(dest, slot_chip, slot_core, source, a):
        block = pl.ds(a * rows, rows)
        return pltpu.make_async_remote_copy(
            src_ref=send2.at[dest, :, block, :],
            dst_ref=recv2.at[slot_chip, :, block, pl.ds(pl.multiple_of(slot_core * lanes, lanes), lanes)],
            send_sem=ss2.at[dest, a], recv_sem=rs2.at[source, a],
            device_id={"row": dest}, device_id_type=MESH)

    loads[2].wait()
    for a in range(2):
        for _, dest in far:
            t = pl.ds(pl.multiple_of(dest * rows, rows), rows)
            result = dot3(inverse[0, a, t, :], inverse[1, a, t, :], coef[0, a], coef[1, a])
            for b in range(2):
                send2[dest, b, pl.ds(a * rows, rows), :] = result[:, b * lanes:(b + 1) * lanes]
            send2_copy(dest, chip, core, me, a).start()
    slot = pl.ds(pl.multiple_of(core * lanes, lanes), lanes)
    for a in range(2):
        for dest in (sibling, me):
            t = pl.ds(pl.multiple_of(dest * rows, rows), rows)
            result = dot3(inverse[0, a, t, :], inverse[1, a, t, :], coef[0, a], coef[1, a])
            for b in range(2):
                piece = result[:, b * lanes:(b + 1) * lanes]
                if dest is me:
                    recv2[chip, b, pl.ds(a * rows, rows), slot] = piece
                else:
                    send2[dest, b, pl.ds(a * rows, rows), :] = piece
            if dest is not me:
                send2_copy(dest, chip, core, me, a).start()

    loads[3].wait()
    for a in range(2):
        send2_copy(sibling, chip, 1 - core, sibling, a).wait_recv()
    wide_step = 256
    even_lane = (lax.broadcasted_iota(jnp.int32, (rows, wide_step), 1) & 1) == 0
    for stage, c in enumerate([chip] + far_chips):
        for a in range(2):
            if stage:
                for kc in range(CORES):
                    send2_copy(c * CORES + kc, c, kc, c * CORES + kc, a).wait_recv()
            block = pl.ds(a * rows, rows)
            for x in range(0, 2 * pixels, wide_step):
                span = pl.ds(x, wide_step)
                values = []
                for b in range(2):
                    hi, lo = halves(recv2[c, b, block, :])
                    values.append(dot3(hi, lo, last[0, c, :, span], last[1, c, :, span]))
                value = jnp.where(even_lane, values[0], values[1])
                place = pl.ds(a, rows, stride=2)
                for k in range(wide_step // 128):
                    piece = value[:, k * 128:(k + 1) * 128]
                    tile = x // 128 + k
                    if stage:
                        piece = piece + woven[tile, place, :]
                    woven[tile, place, :] = piece
    for tile in range(2 * pixels // 128):
        out[:, pl.ds(tile * 128, 128)] = woven[tile]

    for peer in others:
        tot_copy(peer, me).wait_send()
        for g in range(len(groups)):
            send1_copy(peer, chip, core, me, g).wait_send()
        for a in range(2):
            send2_copy(peer, chip, core, me, a).wait_send()


def solution(mesh):
    count = mesh.shape["row"]

    def per_device(frames, phase_offset, order_gain, band_shift):
        phases, rows, pixels = frames.shape[1:]
        lanes = pixels // count
        chips = count // CORES
        lead, column, inverse, last = tables(pixels, count)
        vmem = pl.BlockSpec(memory_space=pltpu.VMEM)
        smem = pl.BlockSpec(memory_space=pltpu.SMEM)
        hbm = pl.BlockSpec(memory_space=pl.ANY)
        bf16, f32 = jnp.bfloat16, jnp.float32
        dma = pltpu.SemaphoreType.DMA
        return pl.pallas_call(
            functools.partial(kernel, count, otf_polynomial()),
            out_shape=pltpu.VMEM((2 * rows, 2 * pixels), f32),
            in_specs=[vmem, smem, smem, smem, hbm, hbm, hbm, hbm],
            out_specs=vmem,
            scratch_shapes=[
                pltpu.VMEM(lead.shape, bf16),
                pltpu.VMEM(column.shape, bf16),
                pltpu.VMEM(inverse.shape, bf16),
                pltpu.VMEM(last.shape, bf16),
                pltpu.VMEM((8, 128), f32),
                pltpu.VMEM((count, 8, 128), f32),
                pltpu.VMEM((2, phases * rows, pixels), bf16),
                pltpu.VMEM((count, rows, phases * lanes), f32),
                pltpu.VMEM((chips, CORES * rows, phases * lanes), f32),
                pltpu.VMEM((pixels, phases * lanes), f32),
                pltpu.VMEM((phases // 2 + 1, 2, pixels // 2, lanes), f32),
                pltpu.VMEM((2, 2, pixels, 2 * lanes), bf16),
                pltpu.VMEM((count, 2, 2 * rows, lanes), f32),
                pltpu.VMEM((chips, 2, 2 * rows, CORES * lanes), f32),
                pltpu.VMEM((2 * pixels // 128, 2 * rows, 128), f32),
                dma((4,)),
                dma((count,)), dma((count,)),
                dma((count, 3)), dma((count, 3)),
                dma((count, 2)), dma((count, 2)),
            ],
            compiler_params=pltpu.CompilerParams(
                collective_id=0, has_side_effects=True, vmem_limit_bytes=60000000
            ),
        )(frames, phase_offset, order_gain, band_shift,
          jnp.asarray(lead), jnp.asarray(column), jnp.asarray(inverse), jnp.asarray(last))

    in_specs = (P("fov", None, "row", None), P("fov"), P("fov", None), P("fov", None))
    return jax.shard_map(
        per_device, mesh=mesh, in_specs=in_specs, out_specs=P(("fov", "row"), None), check_vma=False
    )
```

profile of v0, /device:TPU:0, one launch (start us, length us, event | category | flops | bytes accessed | tf_op | source)
XLA Modules:
  0.0 41.7 jit_solution(16394480259338583060)
XLA Ops:
  0.7 40.1 %shard_map.82 = f32[256,1024]{1,0:T(8,128)S(1)} custom-call(bf16[1,5,128,512]{3,2,1,0:T(8,128)(2,1)} %frames.1, f32[1]{0:T(128)S(6)} %copy.11.offset, f32[1,5]{1,0:T(1,128)} %gain.1, s32[1,2]{1,0:T(1,128)} %shift.1, bf16[2,2,512,256]{3,2,1,0:T(8,128)(2,1)} %constant.8.clone.lead_h, bf16[2,2,512,256]{3,2,1,0:T(8,128)(2,1)} %constant.9.clone.column_h, ...), custom_call_target="tpu_custom_call" | custom-call | tf_op jit(solution)/shard_map/pallas_call | solution.py:466
  40.8 1.0 %copy.10 = f32[256,1024]{1,0:T(8,128)} copy(f32[256,1024]{1,0:T(8,128)S(1)} %shard_map.82) | data formatting | bytes 2097152
where the time goes:
time: 42.3 us; the launch traced here: 41.7 us
  Pallas kernels  40.1 us (95%)
  local copies, waits for them, and re-layouts  0.97 us (2%)
  between operations  0.66 us (2%)
    pallas_call x1, Pallas kernels, per_device(): pl.pallas_call(functools.partial(kernel, count, otf_polynomial()), out_sh...  40.1 us
    unnamed x1, local copies, waits for them, and re-layouts  0.97 us

commit v1 on v0

v1 whole, which is shorter than its diff:
```python
import functools
import math

import jax
import jax.numpy as jnp
import numpy as np
from jax import lax
from jax.experimental import pallas as pl
from jax.experimental.pallas import tpu as pltpu
from jax.sharding import PartitionSpec as P

MESH = pl.DeviceIdType.MESH
wiener = 0.1
gain_out = 8.0
cut_share = 0.45
CORES = 2
STEP = 16


def max_shift(pixels):
    return 3 * pixels // 16


def split_table(table):
    high = table.astype(np.float32).astype(jnp.bfloat16)
    low = (table - high.astype(np.float64)).astype(np.float32).astype(jnp.bfloat16)
    return np.stack([high, low])


def cos_sin(points, freqs, length):
    angle = 2.0 * math.pi * ((points[:, None] * freqs[None, :]) % length) / length
    return np.cos(angle), np.sin(angle)


def lane_order(wide):
    drop = wide // 4
    return np.concatenate([np.arange(1, drop + 1), [0], np.arange(drop + 1, wide)])


def tables(pixels, count):
    half = pixels // 2
    wide = half // CORES
    chips = count // CORES
    drop = wide // 4
    points = np.arange(pixels)
    freqs = np.arange(half)
    alternate = 1.0 - 2.0 * (points % 2)
    cos_f, sin_f = cos_sin(points, freqs, pixels)
    sin_f[:, 0] = alternate
    column = np.concatenate([cos_f, sin_f], axis=1).T
    column = column.reshape(pixels, chips, pixels // chips).transpose(1, 0, 2)
    inverse = []
    for odd in range(2):
        cos_i, sin_i = cos_sin(2 * points + odd, freqs, 2 * pixels)
        sin_i[:, 0] = alternate
        inverse.append(np.concatenate([cos_i, sin_i], axis=1))
    inverse = np.stack(inverse)
    lead, last = [], []
    places = np.arange(2 * pixels)
    for core in range(CORES):
        own = CORES * lane_order(wide) + core
        lead.append(np.concatenate([cos_f[:, own], sin_f[:, own]], axis=1))
        near_cos, near_sin = cos_sin(places, own, 2 * pixels)
        share = np.where(own == 0, 1.0, 2.0)
        near = np.concatenate([(near_cos * share).T, (-near_sin * share).T])
        mirror = np.where(own == 0, half, pixels - own)
        assert (pixels - own[:drop]).min() > cut_share * pixels + 2 * max_shift(pixels)
        far_cos, far_sin = cos_sin(places, mirror, 2 * pixels)
        keep = np.where(np.arange(wide) < drop, 0.0, 2.0)
        far = np.concatenate([(far_cos * keep).T, (-far_sin * keep).T])
        last.append(np.stack([near, far]))
    return tuple(split_table(t) for t in (np.stack(lead), column, inverse, np.stack(last)))


def otf_polynomial():
    nodes = 0.5 + 0.5 * np.cos(math.pi * (np.arange(64) + 0.5) / 64)
    nodes = np.minimum(nodes, 0.9985)
    root = np.sqrt(1 - nodes * nodes)
    values = 2 / math.pi * (np.arccos(nodes) - nodes * root) / root**3
    fit = np.polynomial.chebyshev.Chebyshev.fit(nodes, values, 9, domain=[0, 1])
    poly = fit.convert(kind=np.polynomial.Polynomial).coef
    return [float(c) for c in poly[::-1]]


def halves(value):
    high = value.astype(jnp.bfloat16)
    return high, (value - high.astype(jnp.float32)).astype(jnp.bfloat16)


def dot(left, right):
    return jnp.dot(left, right, preferred_element_type=jnp.float32)


def dot3(left_hi, left_lo, right_hi, right_lo):
    return dot(left_hi, right_hi) + (dot(left_hi, right_lo) + dot(left_lo, right_hi))


def kernel(count, poly, frames_h, offset, gain, shift, lead_h, column_h, inverse_h, last_h, out,
           frames, lead, column, inverse, last, tot_send, tot, planes, send1, recv1, mixed, alpha, coef,
           near_send, near, send_a, recv_a, send_b, recv_b, part, woven,
           frame_sem, table_sem, tot_ss, tot_rs, ss1, rs1, near_ss, near_rs, a_ss, a_rs, b_ss, b_rs):
    me = lax.axis_index("row")
    chips = count // CORES
    chip, core = me // CORES, me % CORES
    sib_core = 1 - core
    phases, rows, pixels = frames.shape
    half = pixels // 2
    wide = half // CORES
    drop = wide // 4
    orders = phases // 2
    mid = phases // 2
    others = [lax.rem(me + step, count) for step in range(1, count)]
    far_chips = [lax.rem(chip + step, chips) for step in range(1, chips)]
    sibling = chip * CORES + sib_core

    barrier = pltpu.get_barrier_semaphore()
    for peer in others:
        pl.semaphore_signal(barrier, inc=1, device_id={"row": peer}, device_id_type=MESH)
    frame_loads = []
    for p in range(phases):
        frame_loads.append(pltpu.make_async_copy(frames_h.at[0, p], frames.at[p], frame_sem.at[p]))
        frame_loads[p].start()
    loads = []
    for idx, (source, target) in enumerate(
        ((lead_h, lead), (column_h.at[:, chip], column), (inverse_h, inverse), (last_h, last))
    ):
        loads.append(pltpu.make_async_copy(source, target, table_sem.at[idx]))
    loads[0].start()

    lane8 = lax.broadcasted_iota(jnp.int32, (8, 128), 1)
    total_part = jnp.zeros((8, 128), jnp.float32)
    for p in range(phases):
        frame_loads[p].wait()
        f = frames[p].astype(jnp.float32)
        s = jnp.sum(jnp.sum(f, axis=0, keepdims=True), axis=1, keepdims=True)
        total_part = total_part + jnp.where(lane8 == p, s, 0.0)
    tot_send[...] = total_part
    tot[me] = total_part
    pl.semaphore_wait(barrier, count - 1)

    def tot_copy(peer, slot):
        return pltpu.make_async_remote_copy(
            src_ref=tot_send, dst_ref=tot.at[slot], send_sem=tot_ss.at[peer], recv_sem=tot_rs.at[slot],
            device_id={"row": peer}, device_id_type=MESH)

    for peer in others:
        tot_copy(peer, me).start()
    for load in loads[1:]:
        load.start()

    shift_y, shift_x = shift[0, 0], shift[0, 1]
    inv_cut = 1.0 / (cut_share * pixels)
    scale_out = 0.5 * gain_out / (4.0 * pixels * pixels)
    gains = [gain[0, j] for j in range(phases)]
    squares = [g * g for g in gains]
    scaled = [g * scale_out for g in gains]
    reach = int(cut_share * pixels) + 1 + 2 * max_shift(pixels)
    single = (pixels - reach) // STEP

    def own_freq(shape):
        lane = lax.broadcasted_iota(jnp.int32, shape, 1)
        place = jnp.where(lane < drop, lane + 1, jnp.where(lane == drop, 0, lane))
        return CORES * place + core

    def make_alpha(side):
        freq = own_freq((STEP, wide))
        if side:
            freq = jnp.where(freq == 0, half, pixels - freq)
        used = [j for j in range(phases) if not (side and j == mid)]
        sq_xs = {}
        for j in used:
            fx = (freq - (j - mid) * shift_x).astype(jnp.float32) * inv_cut
            sq_xs[j] = fx * fx + 1e-30
        offs = {j: ((j - mid) * shift_y).astype(jnp.float32) * inv_cut for j in used}

        def block(first, slots, top):
            row = first + lax.broadcasted_iota(jnp.int32, (STEP, wide), 0)
            for slot in slots:
                big_y = row if slot % 2 == 0 else -row
                if top and slot % 2:
                    big_y = jnp.where(row == 0, -half, big_y)
                if slot == 2:
                    big_y = big_y - pixels
                if slot == 3:
                    big_y = big_y + pixels
                unit_y = big_y.astype(jnp.float32) * inv_cut
                den = jnp.full((STEP, wide), wiener, jnp.float32)
                den_m = jnp.full((STEP, wide), wiener, jnp.float32)
                values = {}
                for j in used:
                    fy = unit_y - offs[j]
                    t = fy * fy + sq_xs[j]
                    r = t * lax.rsqrt(t)
                    u = jnp.maximum(1.0 - t, 1e-30)
                    v = u * lax.rsqrt(u)
                    acc = poly[0] * r + poly[1]
                    for c in poly[2:]:
                        acc = acc * r + c
                    value = acc * (u * v)
                    values[j] = value
                    sq = value * value
                    den = den + squares[j] * sq
                    den_m = den_m + squares[phases - 1 - j] * sq
                both = 1.0 / (den * den_m)
                inv, inv_m = den_m * both, den * both
                for j in used:
                    alpha[side, slot, j, pl.ds(first, STEP), :] = values[j] * (
                        scaled[j] * inv + scaled[phases - 1 - j] * inv_m)

        block(0, (0, 1, 2, 3), True)

        def few(i, carry):
            block(pl.multiple_of(i * STEP, STEP), (0, 1), False)
            return carry

        def many(i, carry):
            block(pl.multiple_of(i * STEP, STEP), (0, 1, 2, 3), False)
            return carry

        lax.fori_loop(1, max(single, 1), few, 0)
        lax.fori_loop(max(single, 1), half // STEP, many, 0)

    turn = 2.0 * math.pi / pixels

    def ramp(points, step):
        arg = ((points * step) & (pixels - 1)).astype(jnp.float32) * turn
        return jnp.cos(arg), jnp.sin(arg)

    def times(left, right):
        return left[0] * right[0] - left[1] * right[1], left[0] * right[1] + left[1] * right[0]

    row8 = lax.broadcasted_iota(jnp.int32, (8, 128), 0) + me * rows
    wave_x = [ramp(lane8 + 128 * k, shift_x) for k in range(pixels // 128)]
    base = ramp(row8, shift_y)
    leap = ramp(jnp.full((8, 128), 8, jnp.int32), shift_y)
    pieces = [base]
    for k in range(1, rows // 8):
        pieces.append(times(pieces[-1], leap))
    wave_y = tuple(jnp.concatenate([q[k] for q in pieces], axis=0) for k in range(2))
    waves = {1: (wave_y, wave_x)}
    for order in range(2, orders + 1):
        last_y, last_x = waves[order - 1]
        waves[order] = (times(last_y, wave_y), [times(a, b) for a, b in zip(last_x, wave_x)])
    angle = 2.0 * math.pi / phases * lane8.astype(jnp.float32) + offset[0]
    unmix = {order: (jnp.cos(order * angle), jnp.sin(order * angle)) for order in range(1, orders + 1)}

    make_alpha(0)

    for peer in others:
        tot_copy(peer, peer).wait_recv()
    total = tot[0]
    for d in range(1, count):
        total = total + tot[d]
    level = jnp.where(lane8 < phases, float(pixels * pixels), 0.0) / jnp.where(lane8 < phases, total, 1.0)
    level = level / phases

    groups = [(4 * g, 4, g + 1) for g in range(orders)] + [(4 * orders, 2, 0)]

    def send1_copy(slot_core, g):
        first, tiles, _ = groups[g]
        window = pl.ds(first * wide, tiles * wide)
        return pltpu.make_async_remote_copy(
            src_ref=send1.at[:, window],
            dst_ref=recv1.at[pl.ds(pl.multiple_of(slot_core * rows, rows), rows), window],
            send_sem=ss1.at[g], recv_sem=rs1.at[g],
            device_id={"row": sibling}, device_id_type=MESH)

    def spectrum_lines(g, place, target_core, write):
        first, tiles, order = groups[g]
        span = pl.ds(place * rows, (2 if order else 1) * rows)
        result = dot3(planes[0, span, :], planes[1, span, :], lead[0, target_core], lead[1, target_core])
        special = jnp.logical_and(
            lax.broadcasted_iota(jnp.int32, (rows, wide), 1) == drop, target_core == 0)
        if order:
            cr, sr = result[:rows, :wide], result[:rows, wide:]
            ci, si = result[rows:, :wide], result[rows:, wide:]
            values = [jnp.where(special, cr, cr + si), jnp.where(special, ci, ci - sr),
                      jnp.where(special, sr, cr - si), jnp.where(special, si, ci + sr)]
        else:
            values = [result[:, :wide], jnp.where(special, 0.0, -result[:, wide:])]
        for k, value in enumerate(values):
            write(pl.ds((first + k) * wide, wide), value)

    def write_send(window, value):
        send1[:, window] = value

    mine = pl.ds(pl.multiple_of(core * rows, rows), rows)

    def write_mine(window, value):
        recv1[mine, window] = value

    loads[0].wait()
    places = [2 * g if groups[g][2] else 2 * orders for g in range(len(groups))]
    for g, (first, tiles, order) in enumerate(groups):
        coef_re, coef_im = level, None
        if order:
            coef_re, coef_im = level * unmix[order][0], -level * unmix[order][1]
        for x in range(pixels // 128):
            span = pl.ds(x * 128, 128)
            bands = [None, None]
            for p in range(phases):
                f = frames[p, :, span].astype(jnp.float32)
                for k, coefs in enumerate((coef_re, coef_im)):
                    if coefs is None:
                        continue
                    term = coefs[:1, p:p + 1] * f
                    bands[k] = term if bands[k] is None else bands[k] + term
            if order:
                wy, wx = waves[order][0], waves[order][1][x]
                ramps = times(wy, (wx[0][:1], wx[1][:1]))
                bands = times(bands, ramps)
            for k, value in enumerate(bands[:2 if order else 1]):
                hi, lo = halves(value)
                planes[0, pl.ds((places[g] + k) * rows, rows), span] = hi
                planes[1, pl.ds((places[g] + k) * rows, rows), span] = lo
        spectrum_lines(g, places[g], sib_core, write_send)
        send1_copy(core, g).start()
    for g in range(len(groups)):
        spectrum_lines(g, places[g], core, write_mine)

    loads[1].wait()
    for g, (first, tiles, order) in enumerate(groups):
        window = pl.ds(first * wide, tiles * wide)
        send1_copy(sib_core, g).wait_recv()
        hi, lo = halves(recv1[:, window])
        mixed[:, window] = dot3(column[0], column[1], hi, lo)

    special = jnp.logical_and(lax.broadcasted_iota(jnp.int32, (STEP, wide), 1) == drop, core == 0)

    def combine(side):
        def block(first, second, top):
            here, below = pl.ds(first, STEP), pl.ds(half + first, STEP)
            row0 = None
            if top:
                row0 = lax.broadcasted_iota(jnp.int32, (STEP, wide), 0) == 0

            def pick(at_top, value):
                return jnp.where(row0, at_top, value) if top else value

            def signs(tile):
                re, im = pl.ds(tile * wide, wide), pl.ds((tile + 1) * wide, wide)
                cr, ci, sr, si = mixed[here, re], mixed[here, im], mixed[below, re], mixed[below, im]
                plus = (pick(cr, cr + si), pick(ci, ci - sr))
                minus = (pick(sr, cr - si), pick(si, ci + sr))
                return plus, minus

            slots = (0, 1, 2, 3) if second else (0, 1)
            sums = {slot: [None, None] for slot in slots}

            def add(slot, k, term):
                sums[slot][k] = term if sums[slot][k] is None else sums[slot][k] + term

            if side == 0:
                center = signs(4 * orders)
                for slot in slots:
                    a = alpha[side, slot, mid, here, :]
                    for k in range(2):
                        add(slot, k, a * center[slot % 2][k])
            for order in range(1, orders + 1):
                pos, neg = signs(4 * (order - 1)), signs(4 * (order - 1) + 2)
                direct, other = (pos, neg) if side == 0 else (neg, pos)
                partner = [[jnp.where(special, direct[s][k], other[s][k]) for k in range(2)] for s in range(2)]
                if top:
                    swap = [[pick(partner[s][k], partner[1 - s][k]) for k in range(2)] for s in range(2)]
                else:
                    swap = [partner[1], partner[0]]
                for slot in slots:
                    s = slot % 2
                    up, down = alpha[side, slot, mid + order, here, :], alpha[side, slot, mid - order, here, :]
                    add(slot, 0, up * direct[s][0] + down * swap[s][0])
                    add(slot, 1, up * direct[s][1] - down * swap[s][1])
            for a in range(2):
                def folded(s, k):
                    if not second:
                        return sums[s][k]
                    return sums[s][k] + sums[2 + s][k] if a == 0 else sums[s][k] - sums[2 + s][k]

                pr, pi, mr, mi = folded(0, 0), folded(0, 1), folded(1, 0), folded(1, 1)
                low_top = (mr, mi) if a == 0 else (mi, -mr)
                values = [(here, 0, pick(pr, pr + mr)), (here, 1, pick(pi, pi + mi)),
                          (below, 0, pick(low_top[0], mi - pi)), (below, 1, pick(low_top[1], pr - mr))]
                for place, k, value in values:
                    hi, lo = halves(value)
                    coef[0, side, a, place, pl.ds(k * wide, wide)] = hi
                    coef[1, side, a, place, pl.ds(k * wide, wide)] = lo

        block(0, True, True)

        def few(i, carry):
            block(pl.multiple_of(i * STEP, STEP), False, False)
            return carry

        def many(i, carry):
            block(pl.multiple_of(i * STEP, STEP), True, False)
            return carry

        lax.fori_loop(1, max(single, 1), few, 0)
        lax.fori_loop(max(single, 1), half // STEP, many, 0)

    def to_rows(side, a, first_row, length):
        t = pl.ds(pl.multiple_of(first_row, rows), length)
        return dot3(inverse[0, a, t, :], inverse[1, a, t, :], coef[0, side, a], coef[1, side, a])

    def a_copy(c, kc, slot_chip, slot_core, a):
        return pltpu.make_async_remote_copy(
            src_ref=send_a.at[c, a, pl.ds(kc * rows, rows), :], dst_ref=recv_a.at[slot_chip, slot_core, a],
            send_sem=a_ss.at[c, kc, a], recv_sem=a_rs.at[slot_chip, slot_core, a],
            device_id={"row": c * CORES + kc}, device_id_type=MESH)

    def b_copy(c, kc, slot_chip, slot_core, a):
        return pltpu.make_async_remote_copy(
            src_ref=send_b.at[c, kc, a], dst_ref=recv_b.at[slot_chip, slot_core, a],
            send_sem=b_ss.at[c, kc, a], recv_sem=b_rs.at[slot_chip, slot_core, a],
            device_id={"row": c * CORES + kc}, device_id_type=MESH)

    def near_copy(slot_core, side, a):
        return pltpu.make_async_remote_copy(
            src_ref=near_send.at[side, a], dst_ref=near.at[slot_core, side, a],
            send_sem=near_ss.at[side, a], recv_sem=near_rs.at[side, a],
            device_id={"row": sibling}, device_id_type=MESH)

    combine(0)
    loads[2].wait()
    for c in far_chips:
        for a in range(2):
            send_a[c, a] = to_rows(0, a, c * CORES * rows, CORES * rows)
            for kc in range(CORES):
                a_copy(c, kc, chip, core, a).start()

    make_alpha(1)
    combine(1)
    quarter = rows // 4
    lane_q = lax.broadcasted_iota(jnp.int32, (quarter, wide), 1)
    for c in far_chips:
        for a in range(2):
            result = to_rows(1, a, c * CORES * rows, CORES * rows)
            for kc in range(CORES):
                for k in range(2):
                    piece = result[kc * rows:(kc + 1) * rows, k * wide:(k + 1) * wide]
                    tail = piece[3 * quarter:]
                    for i in range(3):
                        moved = pltpu.roll(tail, wide - drop * (i + 1), 1)
                        send_b[c, kc, a, pl.ds(i * quarter, quarter), pl.ds(k * wide, wide)] = jnp.where(
                            lane_q < drop, moved, piece[i * quarter:(i + 1) * quarter])
                b_copy(c, kc, chip, core, a).start()

    for side in range(2):
        for a in range(2):
            near_send[side, a] = to_rows(side, a, sibling * rows, rows)
            near_copy(core, side, a).start()
    for side in range(2):
        for a in range(2):
            near[core, side, a] = to_rows(side, a, me * rows, rows)

    loads[3].wait()
    chunk = 256
    for side in range(2):
        for a in range(2):
            near_copy(sib_core, side, a).wait_recv()

    def finish(a, side, pieces, write):
        split = [halves(piece) for piece in pieces]
        for x in range(0, 2 * pixels, chunk):
            span = pl.ds(x, chunk)
            value = None
            for k, (hi, lo) in enumerate(split):
                term = dot3(hi, lo, last[0, k, side, :, span], last[1, k, side, :, span])
                value = term if value is None else value + term
            write(a, x, value)

    def write_part(a, x, value):
        part[a, :, pl.ds(x, chunk)] = value

    def write_out(a, x, value):
        value = value + part[a, :, pl.ds(x, chunk)]
        for k in range(chunk // 128):
            woven[x // 128 + k, pl.ds(a, rows, stride=2), :] = value[:, k * 128:(k + 1) * 128]

    for a in range(2):
        pieces = []
        for k in range(CORES):
            value = near[k, 0, a]
            for c in far_chips:
                a_copy(c, k, c, k, a).wait_recv()
                value = value + recv_a[c, k, a]
            pieces.append(value)
        finish(a, 0, pieces, write_part)

    def unpacked(c, k, a):
        sides = []
        for q in range(2):
            lanes = pl.ds(q * wide, wide)
            packed = [recv_b[c, k, a, pl.ds(i * quarter, quarter), lanes] for i in range(3)]
            tail = pltpu.roll(packed[2], 3 * drop, 1)
            for i in (1, 0):
                tail = jnp.where(lane_q < (i + 2) * drop, pltpu.roll(packed[i], (i + 1) * drop, 1), tail)
            sides.append(jnp.concatenate(packed + [tail], axis=0))
        return jnp.concatenate(sides, axis=1)

    for a in range(2):
        pieces = []
        for k in range(CORES):
            value = near[k, 1, a]
            for c in far_chips:
                b_copy(c, k, c, k, a).wait_recv()
                value = value + unpacked(c, k, a)
            pieces.append(value)
        finish(a, 1, pieces, write_out)
    for tile in range(2 * pixels // 128):
        out[:, pl.ds(tile * 128, 128)] = woven[tile]

    for peer in others:
        tot_copy(peer, me).wait_send()
    for g in range(len(groups)):
        send1_copy(core, g).wait_send()
    for a in range(2):
        for side in range(2):
            near_copy(core, side, a).wait_send()
        for c in far_chips:
            for kc in range(CORES):
                a_copy(c, kc, chip, core, a).wait_send()
                b_copy(c, kc, chip, core, a).wait_send()


def solution(mesh):
    count = mesh.shape["row"]

    def per_device(frames, phase_offset, order_gain, band_shift):
        phases, rows, pixels = frames.shape[1:]
        chips = count // CORES
        half = pixels // 2
        wide = half // CORES
        tiles = 4 * (phases // 2) + 2
        lead, column, inverse, last = tables(pixels, count)
        vmem = pl.BlockSpec(memory_space=pltpu.VMEM)
        smem = pl.BlockSpec(memory_space=pltpu.SMEM)
        hbm = pl.BlockSpec(memory_space=pl.ANY)
        bf16, f32 = jnp.bfloat16, jnp.float32
        dma = pltpu.SemaphoreType.DMA
        return pl.pallas_call(
            functools.partial(kernel, count, otf_polynomial()),
            out_shape=pltpu.VMEM((2 * rows, 2 * pixels), f32),
            in_specs=[hbm, smem, smem, smem, hbm, hbm, hbm, hbm],
            out_specs=vmem,
            scratch_shapes=[
                pltpu.VMEM((phases, rows, pixels), bf16),
                pltpu.VMEM(lead.shape, bf16),
                pltpu.VMEM((2, pixels, CORES * rows), bf16),
                pltpu.VMEM(inverse.shape, bf16),
                pltpu.VMEM(last.shape, bf16),
                pltpu.VMEM((8, 128), f32),
                pltpu.VMEM((count, 8, 128), f32),
                pltpu.VMEM((2, phases * rows, pixels), bf16),
                pltpu.VMEM((rows, tiles * wide), f32),
                pltpu.VMEM((CORES * rows, tiles * wide), f32),
                pltpu.VMEM((pixels, tiles * wide), f32),
                pltpu.VMEM((2, 4, phases, half, wide), f32),
                pltpu.VMEM((2, 2, 2, pixels, 2 * wide), bf16),
                pltpu.VMEM((2, 2, rows, 2 * wide), f32),
                pltpu.VMEM((CORES, 2, 2, rows, 2 * wide), f32),
                pltpu.VMEM((chips, 2, CORES * rows, 2 * wide), f32),
                pltpu.VMEM((chips, CORES, 2, rows, 2 * wide), f32),
                pltpu.VMEM((chips, CORES, 2, 3 * rows // 4, 2 * wide), f32),
                pltpu.VMEM((chips, CORES, 2, 3 * rows // 4, 2 * wide), f32),
                pltpu.VMEM((2, rows, 2 * pixels), f32),
                pltpu.VMEM((2 * pixels // 128, 2 * rows, 128), f32),
                dma((phases,)), dma((4,)),
                dma((count,)), dma((count,)),
                dma((phases // 2 + 1,)), dma((phases // 2 + 1,)),
                dma((2, 2)), dma((2, 2)),
                dma((chips, CORES, 2)), dma((chips, CORES, 2)),
                dma((chips, CORES, 2)), dma((chips, CORES, 2)),
            ],
            compiler_params=pltpu.CompilerParams(
                collective_id=0, has_side_effects=True, vmem_limit_bytes=60000000
            ),
        )(frames, phase_offset, order_gain, band_shift,
          jnp.asarray(lead), jnp.asarray(column), jnp.asarray(inverse), jnp.asarray(last))

    in_specs = (P("fov", None, "row", None), P("fov"), P("fov", None), P("fov", None))
    return jax.shard_map(
        per_device, mesh=mesh, in_specs=in_specs, out_specs=P(("fov", "row"), None), check_vma=False
    )
```

time: 42.3 us -> 37.5 us (0.89)
  the two profiles are of different devices: /device:TPU:0 before, /device:TPU:1 now
where the time goes in v1:
time: 37.5 us; the launch traced here: 37.3 us
  Pallas kernels  35.7 us (95%)
  local copies, waits for them, and re-layouts  0.97 us (3%)
  between operations  0.66 us (2%)
    pallas_call x1, Pallas kernels, per_device(): pl.pallas_call(functools.partial(kernel, count, otf_polynomial()), out_sh...  35.7 us
    unnamed x1, local copies, waits for them, and re-layouts  0.97 us

profile of v1, /device:TPU:1, one launch (start us, length us, event | category | flops | bytes accessed | tf_op | source)
XLA Modules:
  0.0 37.3 jit_solution(12542103768920684709)
XLA Ops:
  0.7 35.7 %shard_map.82 = f32[256,1024]{1,0:T(8,128)S(1)} custom-call(bf16[1,5,128,512]{3,2,1,0:T(8,128)(2,1)} %frames_h.1, f32[1]{0:T(128)S(6)} %copy.11.offset, f32[1,5]{1,0:T(1,128)} %gain.1, s32[1,2]{1,0:T(1,128)} %shift.1, bf16[2,2,512,256]{3,2,1,0:T(8,128)(2,1)} %constant.8.clone.lead_h, bf16[2,2,512,256]{3,2,1,0:T(8,128)(2,1)} %constant.9.clone.column_h, ...), custom_call_target="tpu_custom_call" | custom-call | tf_op jit(solution)/shard_map/pallas_call | solution.py:540
  36.3 1.0 %copy.10 = f32[256,1024]{1,0:T(8,128)} copy(f32[256,1024]{1,0:T(8,128)S(1)} %shard_map.82) | data formatting | bytes 2097152

commit v2 on v1

--- a/solution.py
+++ b/solution.py
@@ -47,19 +47,21 @@
     alternate = 1.0 - 2.0 * (points % 2)
     cos_f, sin_f = cos_sin(points, freqs, pixels)
     sin_f[:, 0] = alternate
-    column = np.concatenate([cos_f, sin_f], axis=1).T
+    parities = [np.arange(q, half, 2) for q in range(2)]
+    order = np.concatenate(parities)
+    column = np.concatenate([cos_f[:, order], sin_f[:, order]], axis=1).T
     column = column.reshape(pixels, chips, pixels // chips).transpose(1, 0, 2)
     inverse = []
     for odd in range(2):
-        cos_i, sin_i = cos_sin(2 * points + odd, freqs, 2 * pixels)
-        sin_i[:, 0] = alternate
-        inverse.append(np.concatenate([cos_i, sin_i], axis=1))
+        cos_i, sin_i = cos_sin(2 * points[:half] + odd, freqs, 2 * pixels)
+        sin_i[:, 0] = alternate[:half]
+        inverse.append(np.stack([np.concatenate([cos_i[:, q], sin_i[:, q]], axis=1) for q in parities]))
     inverse = np.stack(inverse)
     lead, last = [], []
-    places = np.arange(2 * pixels)
+    places = np.arange(pixels)
     for core in range(CORES):
         own = CORES * lane_order(wide) + core
-        lead.append(np.concatenate([cos_f[:, own], sin_f[:, own]], axis=1))
+        lead.append(np.concatenate([cos_f[:half, own], sin_f[:half, own]], axis=1))
         near_cos, near_sin = cos_sin(places, own, 2 * pixels)
         share = np.where(own == 0, 1.0, 2.0)
         near = np.concatenate([(near_cos * share).T, (-near_sin * share).T])
@@ -96,9 +98,9 @@
 
 
 def kernel(count, poly, frames_h, offset, gain, shift, lead_h, column_h, inverse_h, last_h, out,
-           frames, lead, column, inverse, last, tot_send, tot, planes, send1, recv1, mixed, alpha, coef,
+           frames, lead, column, inverse, last, tot_send, tot, folds, ramps, planes, spec, mixed, alpha, coef,
            near_send, near, send_a, recv_a, send_b, recv_b, part, woven,
-           frame_sem, table_sem, tot_ss, tot_rs, ss1, rs1, near_ss, near_rs, a_ss, a_rs, b_ss, b_rs):
+           frame_sem, table_sem, tot_ss, tot_rs, fold_ss, fold_rs, near_ss, near_rs, a_ss, a_rs, b_ss, b_rs):
     me = lax.axis_index("row")
     chips = count // CORES
     chip, core = me // CORES, me % CORES
@@ -122,17 +124,21 @@
         frame_loads[p].start()
     loads = []
     for idx, (source, target) in enumerate(
-        ((lead_h, lead), (column_h.at[:, chip], column), (inverse_h, inverse), (last_h, last))
+        ((lead_h.at[:, core], lead), (column_h.at[:, chip], column), (inverse_h, inverse), (last_h, last))
     ):
         loads.append(pltpu.make_async_copy(source, target, table_sem.at[idx]))
     loads[0].start()
 
+    mine = pl.ds(pl.multiple_of(core * rows, rows), rows)
     lane8 = lax.broadcasted_iota(jnp.int32, (8, 128), 1)
     total_part = jnp.zeros((8, 128), jnp.float32)
     for p in range(phases):
         frame_loads[p].wait()
-        f = frames[p].astype(jnp.float32)
-        s = jnp.sum(jnp.sum(f, axis=0, keepdims=True), axis=1, keepdims=True)
+        lower, upper = frames[p, :, :half].astype(jnp.float32), frames[p, :, half:].astype(jnp.float32)
+        both = lower + upper
+        folds[0, p, mine, :] = both
+        folds[1, p, mine, :] = lower - upper
+        s = jnp.sum(jnp.sum(both, axis=0, keepdims=True), axis=1, keepdims=True)
         total_part = total_part + jnp.where(lane8 == p, s, 0.0)
     tot_send[...] = total_part
     tot[me] = total_part
@@ -145,6 +151,16 @@
 
     for peer in others:
         tot_copy(peer, me).start()
+
+    def fold_copy(slot_core, k):
+        place = pl.ds(pl.multiple_of(slot_core * rows, rows), rows)
+        return pltpu.make_async_remote_copy(
+            src_ref=folds.at[k, :, place], dst_ref=folds.at[k, :, place],
+            send_sem=fold_ss.at[k], recv_sem=fold_rs.at[k],
+            device_id={"row": sibling}, device_id_type=MESH)
+
+    for k in range(2):
+        fold_copy(core, k).start()
     for load in loads[1:]:
         load.start()
 
@@ -155,7 +171,17 @@
     squares = [g * g for g in gains]
     scaled = [g * scale_out for g in gains]
     reach = int(cut_share * pixels) + 1 + 2 * max_shift(pixels)
-    single = (pixels - reach) // STEP
+    single = max((pixels - reach) // 2 // STEP, 1)
+    quarter = half // 2
+
+    def blocks(block, few, many):
+        for odd in range(2):
+            def body(which, i, carry):
+                block(pl.multiple_of(i * STEP, STEP), odd, which, False)
+                return carry
+
+            lax.fori_loop(1 - odd, single, functools.partial(body, few), 0)
+            lax.fori_loop(single, quarter // STEP, functools.partial(body, many), 0)
 
     def own_freq(shape):
         lane = lax.broadcasted_iota(jnp.int32, shape, 1)
@@ -173,8 +199,9 @@
             sq_xs[j] = fx * fx + 1e-30
         offs = {j: ((j - mid) * shift_y).astype(jnp.float32) * inv_cut for j in used}
 
-        def block(first, slots, top):
-            row = first + lax.broadcasted_iota(jnp.int32, (STEP, wide), 0)
+        def block(first, odd, slots, top):
+            row = 2 * (first + lax.broadcasted_iota(jnp.int32, (STEP, wide), 0)) + odd
+            here = pl.ds(odd * quarter + first, STEP)
             for slot in slots:
                 big_y = row if slot % 2 == 0 else -row
                 if top and slot % 2:
@@ -204,21 +231,11 @@
                 both = 1.0 / (den * den_m)
                 inv, inv_m = den_m * both, den * both
                 for j in used:
-                    alpha[side, slot, j, pl.ds(first, STEP), :] = values[j] * (
+                    alpha[side, slot, j, here, :] = values[j] * (
                         scaled[j] * inv + scaled[phases - 1 - j] * inv_m)
 
-        block(0, (0, 1, 2, 3), True)
-
-        def few(i, carry):
-            block(pl.multiple_of(i * STEP, STEP), (0, 1), False)
-            return carry
-
-        def many(i, carry):
-            block(pl.multiple_of(i * STEP, STEP), (0, 1, 2, 3), False)
-            return carry
-
-        lax.fori_loop(1, max(single, 1), few, 0)
-        lax.fori_loop(max(single, 1), half // STEP, many, 0)
+        block(0, 0, (0, 1, 2, 3), True)
+        blocks(block, (0, 1), (0, 1, 2, 3))
 
     turn = 2.0 * math.pi / pixels
 
@@ -229,20 +246,24 @@
     def times(left, right):
         return left[0] * right[0] - left[1] * right[1], left[0] * right[1] + left[1] * right[0]
 
-    row8 = lax.broadcasted_iota(jnp.int32, (8, 128), 0) + me * rows
-    wave_x = [ramp(lane8 + 128 * k, shift_x) for k in range(pixels // 128)]
+    row8 = lax.broadcasted_iota(jnp.int32, (8, 128), 0) + chip * (CORES * rows)
+    wave_x = [ramp(lane8 + 128 * k, shift_x) for k in range(half // 128)]
     base = ramp(row8, shift_y)
     leap = ramp(jnp.full((8, 128), 8, jnp.int32), shift_y)
     pieces = [base]
-    for k in range(1, rows // 8):
+    for k in range(1, CORES * rows // 8):
         pieces.append(times(pieces[-1], leap))
     wave_y = tuple(jnp.concatenate([q[k] for q in pieces], axis=0) for k in range(2))
-    waves = {1: (wave_y, wave_x)}
-    for order in range(2, orders + 1):
-        last_y, last_x = waves[order - 1]
-        waves[order] = (times(last_y, wave_y), [times(a, b) for a, b in zip(last_x, wave_x)])
-    angle = 2.0 * math.pi / phases * lane8.astype(jnp.float32) + offset[0]
-    unmix = {order: (jnp.cos(order * angle), jnp.sin(order * angle)) for order in range(1, orders + 1)}
+    start = jnp.full((8, 128), offset[0], jnp.float32)
+    wave_x = [times(w, (jnp.cos(start), -jnp.sin(start))) for w in wave_x]
+    for k in range(half // 128):
+        turned = times(wave_y, (wave_x[k][0][:1], wave_x[k][1][:1]))
+        value = turned
+        for order in range(orders):
+            if order:
+                value = times(value, turned)
+            for q in range(2):
+                ramps[order, q, :, pl.ds(k * 128, 128)] = value[q]
 
     make_alpha(0)
 
@@ -256,80 +277,78 @@
 
     groups = [(4 * g, 4, g + 1) for g in range(orders)] + [(4 * orders, 2, 0)]
 
-    def send1_copy(slot_core, g):
-        first, tiles, _ = groups[g]
-        window = pl.ds(first * wide, tiles * wide)
-        return pltpu.make_async_remote_copy(
-            src_ref=send1.at[:, window],
-            dst_ref=recv1.at[pl.ds(pl.multiple_of(slot_core * rows, rows), rows), window],
-            send_sem=ss1.at[g], recv_sem=rs1.at[g],
-            device_id={"row": sibling}, device_id_type=MESH)
-
-    def spectrum_lines(g, place, target_core, write):
+    span_rows = CORES * rows
+
+    def scaled_folds(which, rows_at, lanes_at):
+        return [level[:1, p:p + 1] * folds[which, p, rows_at, lanes_at] for p in range(phases)]
+
+    def modulated(order, values, rows_at, lanes_at):
+        re, im = values[0], None
+        for q in range(1, mid + 1):
+            theta = 2.0 * math.pi * order * q / phases
+            re = re + math.cos(theta) * (values[q] + values[phases - q])
+            term = -math.sin(theta) * (values[q] - values[phases - q])
+            im = term if im is None else im + term
+        return times((re, im), [ramps[order - 1, k, rows_at, lanes_at] for k in range(2)])
+
+    swapped = core + (shift_x & 1) * (1 - 2 * core)
+
+    def unmix(wanted):
+        which = swapped if wanted[0] % 2 else core
+        for r in range(0, span_rows, STEP):
+            for x in range(0, half, 128):
+                rows_at, lanes_at = pl.ds(r, STEP), pl.ds(x, 128)
+                values = scaled_folds(which, rows_at, lanes_at)
+                for order in wanted:
+                    if order:
+                        made = modulated(order, values, rows_at, lanes_at)
+                    else:
+                        made = [functools.reduce(lambda a, b: a + b, values)]
+                    for k, value in enumerate(made):
+                        hi, lo = halves(value)
+                        place = (2 * (order - 1) if order else 2 * orders) + k
+                        planes[0, pl.ds(place * span_rows + r, STEP), lanes_at] = hi
+                        planes[1, pl.ds(place * span_rows + r, STEP), lanes_at] = lo
+
+    def spectrum(g):
         first, tiles, order = groups[g]
-        span = pl.ds(place * rows, (2 if order else 1) * rows)
-        result = dot3(planes[0, span, :], planes[1, span, :], lead[0, target_core], lead[1, target_core])
+        place = 2 * (order - 1) if order else 2 * orders
+        span = pl.ds(place * span_rows, (2 if order else 1) * span_rows)
+        result = dot3(planes[0, span, :], planes[1, span, :], lead[0], lead[1])
         special = jnp.logical_and(
-            lax.broadcasted_iota(jnp.int32, (rows, wide), 1) == drop, target_core == 0)
+            lax.broadcasted_iota(jnp.int32, (span_rows, wide), 1) == drop, core == 0)
         if order:
-            cr, sr = result[:rows, :wide], result[:rows, wide:]
-            ci, si = result[rows:, :wide], result[rows:, wide:]
+            cr, sr = result[:span_rows, :wide], result[:span_rows, wide:]
+            ci, si = result[span_rows:, :wide], result[span_rows:, wide:]
             values = [jnp.where(special, cr, cr + si), jnp.where(special, ci, ci - sr),
                       jnp.where(special, sr, cr - si), jnp.where(special, si, ci + sr)]
         else:
             values = [result[:, :wide], jnp.where(special, 0.0, -result[:, wide:])]
         for k, value in enumerate(values):
-            write(pl.ds((first + k) * wide, wide), value)
-
-    def write_send(window, value):
-        send1[:, window] = value
-
-    mine = pl.ds(pl.multiple_of(core * rows, rows), rows)
-
-    def write_mine(window, value):
-        recv1[mine, window] = value
-
-    loads[0].wait()
-    places = [2 * g if groups[g][2] else 2 * orders for g in range(len(groups))]
-    for g, (first, tiles, order) in enumerate(groups):
-        coef_re, coef_im = level, None
-        if order:
-            coef_re, coef_im = level * unmix[order][0], -level * unmix[order][1]
-        for x in range(pixels // 128):
-            span = pl.ds(x * 128, 128)
-            bands = [None, None]
-            for p in range(phases):
-                f = frames[p, :, span].astype(jnp.float32)
-                for k, coefs in enumerate((coef_re, coef_im)):
-                    if coefs is None:
-                        continue
-                    term = coefs[:1, p:p + 1] * f
-                    bands[k] = term if bands[k] is None else bands[k] + term
-            if order:
-                wy, wx = waves[order][0], waves[order][1][x]
-                ramps = times(wy, (wx[0][:1], wx[1][:1]))
-                bands = times(bands, ramps)
-            for k, value in enumerate(bands[:2 if order else 1]):
-                hi, lo = halves(value)
-                planes[0, pl.ds((places[g] + k) * rows, rows), span] = hi
-                planes[1, pl.ds((places[g] + k) * rows, rows), span] = lo
-        spectrum_lines(g, places[g], sib_core, write_send)
-        send1_copy(core, g).start()
-    for g in range(len(groups)):
-        spectrum_lines(g, places[g], core, write_mine)
-
-    loads[1].wait()
-    for g, (first, tiles, order) in enumerate(groups):
+            hi, lo = halves(value)
+            spec[0, :, pl.ds((first + k) * wide, wide)] = hi
+            spec[1, :, pl.ds((first + k) * wide, wide)] = lo
         window = pl.ds(first * wide, tiles * wide)
-        send1_copy(sib_core, g).wait_recv()
-        hi, lo = halves(recv1[:, window])
-        mixed[:, window] = dot3(column[0], column[1], hi, lo)
+        mixed[:, window] = dot3(column[0], column[1], spec[0, :, window], spec[1, :, window])
+
+    for load in loads[:2]:
+        load.wait()
+    for k in range(2):
+        fold_copy(sib_core, k).wait_recv()
+    for order in range(1, orders + 1, 2):
+        unmix([order])
+        spectrum(order - 1)
+    unmix(list(range(2, orders + 1, 2)) + [0])
+    for order in range(2, orders + 1, 2):
+        spectrum(order - 1)
+    spectrum(orders)
 
     special = jnp.logical_and(lax.broadcasted_iota(jnp.int32, (STEP, wide), 1) == drop, core == 0)
 
     def combine(side):
-        def block(first, second, top):
-            here, below = pl.ds(first, STEP), pl.ds(half + first, STEP)
+        def block(first, odd, second, top):
+            here, below = pl.ds(odd * quarter + first, STEP), pl.ds(half + odd * quarter + first, STEP)
+            upper, lower = pl.ds(first, STEP), pl.ds(quarter + first, STEP)
             row0 = None
             if top:
                 row0 = lax.broadcasted_iota(jnp.int32, (STEP, wide), 0) == 0
@@ -377,29 +396,29 @@
 
                 pr, pi, mr, mi = folded(0, 0), folded(0, 1), folded(1, 0), folded(1, 1)
                 low_top = (mr, mi) if a == 0 else (mi, -mr)
-                values = [(here, 0, pick(pr, pr + mr)), (here, 1, pick(pi, pi + mi)),
-                          (below, 0, pick(low_top[0], mi - pi)), (below, 1, pick(low_top[1], pr - mr))]
+                values = [(upper, 0, pick(pr, pr + mr)), (upper, 1, pick(pi, pi + mi)),
+                          (lower, 0, pick(low_top[0], mi - pi)), (lower, 1, pick(low_top[1], pr - mr))]
                 for place, k, value in values:
                     hi, lo = halves(value)
-                    coef[0, side, a, place, pl.ds(k * wide, wide)] = hi
-                    coef[1, side, a, place, pl.ds(k * wide, wide)] = lo
-
-        block(0, True, True)
-
-        def few(i, carry):
-            block(pl.multiple_of(i * STEP, STEP), False, False)
-            return carry
-
-        def many(i, carry):
-            block(pl.multiple_of(i * STEP, STEP), True, False)
-            return carry
-
-        lax.fori_loop(1, max(single, 1), few, 0)
-        lax.fori_loop(max(single, 1), half // STEP, many, 0)
-
-    def to_rows(side, a, first_row, length):
-        t = pl.ds(pl.multiple_of(first_row, rows), length)
-        return dot3(inverse[0, a, t, :], inverse[1, a, t, :], coef[0, side, a], coef[1, side, a])
+                    coef[0, side, a, odd, place, pl.ds(k * wide, wide)] = hi
+                    coef[1, side, a, odd, place, pl.ds(k * wide, wide)] = lo
+
+        block(0, 0, True, True)
+        blocks(block, False, True)
+
+    flip = jnp.where(chip == 0, 1.0, -1.0)
+
+    def to_rows(side, a):
+        even, odd = [dot3(inverse[0, a, q], inverse[1, a, q], coef[0, side, a, q], coef[1, side, a, q])
+                     for q in range(2)]
+        odd = odd * flip
+        return even + odd, even - odd
+
+    def keep_near(side, a, value):
+        first, second = value[:rows], value[rows:]
+        near[core, side, a] = jnp.where(core == 0, first, second)
+        near_send[side, a] = jnp.where(core == 0, second, first)
+        near_copy(core, side, a).start()
 
     def a_copy(c, kc, slot_chip, slot_core, a):
         return pltpu.make_async_remote_copy(
@@ -423,34 +442,29 @@
     loads[2].wait()
     for c in far_chips:
         for a in range(2):
-            send_a[c, a] = to_rows(0, a, c * CORES * rows, CORES * rows)
+            own_rows, far_rows = to_rows(0, a)
+            send_a[c, a] = far_rows
             for kc in range(CORES):
                 a_copy(c, kc, chip, core, a).start()
+            keep_near(0, a, own_rows)
 
     make_alpha(1)
     combine(1)
-    quarter = rows // 4
-    lane_q = lax.broadcasted_iota(jnp.int32, (quarter, wide), 1)
+    fourth = rows // 4
+    lane_q = lax.broadcasted_iota(jnp.int32, (fourth, wide), 1)
     for c in far_chips:
         for a in range(2):
-            result = to_rows(1, a, c * CORES * rows, CORES * rows)
+            own_rows, far_rows = to_rows(1, a)
             for kc in range(CORES):
                 for k in range(2):
-                    piece = result[kc * rows:(kc + 1) * rows, k * wide:(k + 1) * wide]
-                    tail = piece[3 * quarter:]
+                    piece = far_rows[kc * rows:(kc + 1) * rows, k * wide:(k + 1) * wide]
+                    tail = piece[3 * fourth:]
                     for i in range(3):
                         moved = pltpu.roll(tail, wide - drop * (i + 1), 1)
-                        send_b[c, kc, a, pl.ds(i * quarter, quarter), pl.ds(k * wide, wide)] = jnp.where(
-                            lane_q < drop, moved, piece[i * quarter:(i + 1) * quarter])
+                        send_b[c, kc, a, pl.ds(i * fourth, fourth), pl.ds(k * wide, wide)] = jnp.where(
+                            lane_q < drop, moved, piece[i * fourth:(i + 1) * fourth])
                 b_copy(c, kc, chip, core, a).start()
-
-    for side in range(2):
-        for a in range(2):
-            near_send[side, a] = to_rows(side, a, sibling * rows, rows)
-            near_copy(core, side, a).start()
-    for side in range(2):
-        for a in range(2):
-            near[core, side, a] = to_rows(side, a, me * rows, rows)
+            keep_near(1, a, own_rows)
 
     loads[3].wait()
     chunk = 256
@@ -460,13 +474,12 @@
 
     def finish(a, side, pieces, write):
         split = [halves(piece) for piece in pieces]
-        for x in range(0, 2 * pixels, chunk):
+        for x in range(0, pixels, chunk):
             span = pl.ds(x, chunk)
-            value = None
-            for k, (hi, lo) in enumerate(split):
-                term = dot3(hi, lo, last[0, k, side, :, span], last[1, k, side, :, span])
-                value = term if value is None else value + term
-            write(a, x, value)
+            even, odd = [dot3(hi, lo, last[0, k, side, :, span], last[1, k, side, :, span])
+                         for k, (hi, lo) in enumerate(split)]
+            write(a, x, even + odd)
+            write(a, pixels + x, even - odd)
 
     def write_part(a, x, value):
         part[a, :, pl.ds(x, chunk)] = value
@@ -490,7 +503,7 @@
         sides = []
         for q in range(2):
             lanes = pl.ds(q * wide, wide)
-            packed = [recv_b[c, k, a, pl.ds(i * quarter, quarter), lanes] for i in range(3)]
+            packed = [recv_b[c, k, a, pl.ds(i * fourth, fourth), lanes] for i in range(3)]
             tail = pltpu.roll(packed[2], 3 * drop, 1)
             for i in (1, 0):
                 tail = jnp.where(lane_q < (i + 2) * drop, pltpu.roll(packed[i], (i + 1) * drop, 1), tail)
@@ -511,8 +524,8 @@
 
     for peer in others:
         tot_copy(peer, me).wait_send()
-    for g in range(len(groups)):
-        send1_copy(core, g).wait_send()
+    for k in range(2):
+        fold_copy(core, k).wait_send()
     for a in range(2):
         for side in range(2):
             near_copy(core, side, a).wait_send()
@@ -528,6 +541,7 @@
     def per_device(frames, phase_offset, order_gain, band_shift):
         phases, rows, pixels = frames.shape[1:]
         chips = count // CORES
+        assert chips == 2 and CORES == 2
         half = pixels // 2
         wide = half // CORES
         tiles = 4 * (phases // 2) + 2
@@ -544,18 +558,19 @@
             out_specs=vmem,
             scratch_shapes=[
                 pltpu.VMEM((phases, rows, pixels), bf16),
-                pltpu.VMEM(lead.shape, bf16),
+                pltpu.VMEM((2, half, 2 * wide), bf16),
                 pltpu.VMEM((2, pixels, CORES * rows), bf16),
                 pltpu.VMEM(inverse.shape, bf16),
                 pltpu.VMEM(last.shape, bf16),
                 pltpu.VMEM((8, 128), f32),
                 pltpu.VMEM((count, 8, 128), f32),
-                pltpu.VMEM((2, phases * rows, pixels), bf16),
-                pltpu.VMEM((rows, tiles * wide), f32),
-                pltpu.VMEM((CORES * rows, tiles * wide), f32),
+                pltpu.VMEM((2, phases, CORES * rows, half), f32),
+                pltpu.VMEM((phases // 2, 2, CORES * rows, half), f32),
+                pltpu.VMEM((2, phases * CORES * rows, half), bf16),
+                pltpu.VMEM((2, CORES * rows, tiles * wide), bf16),
                 pltpu.VMEM((pixels, tiles * wide), f32),
                 pltpu.VMEM((2, 4, phases, half, wide), f32),
-                pltpu.VMEM((2, 2, 2, pixels, 2 * wide), bf16),
+                pltpu.VMEM((2, 2, 2, 2, half, 2 * wide), bf16),
                 pltpu.VMEM((2, 2, rows, 2 * wide), f32),
                 pltpu.VMEM((CORES, 2, 2, rows, 2 * wide), f32),
                 pltpu.VMEM((chips, 2, CORES * rows, 2 * wide), f32),
@@ -566,7 +581,7 @@
                 pltpu.VMEM((2 * pixels // 128, 2 * rows, 128), f32),
                 dma((phases,)), dma((4,)),
                 dma((count,)), dma((count,)),
-                dma((phases // 2 + 1,)), dma((phases // 2 + 1,)),
+                dma((2,)), dma((2,)),
                 dma((2, 2)), dma((2, 2)),
                 dma((chips, CORES, 2)), dma((chips, CORES, 2)),
                 dma((chips, CORES, 2)), dma((chips, CORES, 2)),

time: 37.5 us -> 35.6 us (0.949)
  Pallas kernels: 35.7 us -> 33.8 us
    pallas_call x1, Pallas kernels: 35.7 us -> 33.8 us  [per_device(): pl.pallas_call(functools.partial(kernel, count, otf_polynomial()), out_sh...]
where the time goes in v2:
time: 35.6 us; the launch traced here: 35.4 us
  Pallas kernels  33.8 us (95%)
  local copies, waits for them, and re-layouts  0.97 us (3%)
  between operations  0.66 us (2%)
    pallas_call x1, Pallas kernels, per_device(): pl.pallas_call(functools.partial(kernel, count, otf_polynomial()), out_sh...  33.8 us
    unnamed x1, local copies, waits for them, and re-layouts  0.97 us

profile of v2, /device:TPU:1, one launch (start us, length us, event | category | flops | bytes accessed | tf_op | source)
XLA Modules:
  0.0 35.4 jit_solution(8971956969886366577)
XLA Ops:
  0.7 33.8 %shard_map.82 = f32[256,1024]{1,0:T(8,128)S(1)} custom-call(bf16[1,5,128,512]{3,2,1,0:T(8,128)(2,1)} %frames_h.1, f32[1]{0:T(128)S(6)} %copy.11.offset, f32[1,5]{1,0:T(1,128)} %gain.1, s32[1,2]{1,0:T(1,128)} %shift.1, bf16[2,2,256,256]{3,2,1,0:T(8,128)(2,1)} %constant.8.clone.lead_h, bf16[2,2,512,256]{3,2,1,0:T(8,128)(2,1)} %constant.9.clone.column_h, ...), custom_call_target="tpu_custom_call" | custom-call | tf_op jit(solution)/shard_map/pallas_call | solution.py:554
  34.5 1.0 %copy.10 = f32[256,1024]{1,0:T(8,128)} copy(f32[256,1024]{1,0:T(8,128)S(1)} %shard_map.82) | data formatting | bytes 2097152

commit v3 on v2

--- a/solution.py
+++ b/solution.py
@@ -33,7 +33,7 @@
 
 
 def lane_order(wide):
-    drop = wide // 4
+    drop = (wide + 1) // 3
     return np.concatenate([np.arange(1, drop + 1), [0], np.arange(drop + 1, wide)])
 
 
@@ -41,7 +41,7 @@
     half = pixels // 2
     wide = half // CORES
     chips = count // CORES
-    drop = wide // 4
+    drop = (wide + 1) // 3
     points = np.arange(pixels)
     freqs = np.arange(half)
     alternate = 1.0 - 2.0 * (points % 2)
@@ -77,9 +77,8 @@
 def otf_polynomial():
     nodes = 0.5 + 0.5 * np.cos(math.pi * (np.arange(64) + 0.5) / 64)
     nodes = np.minimum(nodes, 0.9985)
-    root = np.sqrt(1 - nodes * nodes)
-    values = 2 / math.pi * (np.arccos(nodes) - nodes * root) / root**3
-    fit = np.polynomial.chebyshev.Chebyshev.fit(nodes, values, 9, domain=[0, 1])
+    values = 2 / math.pi * (np.arccos(nodes) - nodes * np.sqrt(1 - nodes * nodes)) / (1 - nodes) ** 1.5
+    fit = np.polynomial.chebyshev.Chebyshev.fit(nodes, values, 6, domain=[0, 1])
     poly = fit.convert(kind=np.polynomial.Polynomial).coef
     return [float(c) for c in poly[::-1]]
 
@@ -97,10 +96,10 @@
     return dot(left_hi, right_hi) + (dot(left_hi, right_lo) + dot(left_lo, right_hi))
 
 
-def kernel(count, poly, frames_h, offset, gain, shift, lead_h, column_h, inverse_h, last_h, out,
-           frames, lead, column, inverse, last, tot_send, tot, folds, ramps, planes, spec, mixed, alpha, coef,
+def kernel(count, poly, frames_h, offset_h, gain_h, shift_h, lead_h, column_h, inverse_h, last_h, out,
+           offset, gain, shift, frames, lead, column, inverse, last, tot_send, tot, folds, ramps, planes, spec, mixed, alpha, coef,
            near_send, near, send_a, recv_a, send_b, recv_b, part, woven,
-           frame_sem, table_sem, tot_ss, tot_rs, fold_ss, fold_rs, near_ss, near_rs, a_ss, a_rs, b_ss, b_rs):
+           small_sem, frame_sem, table_sem, tot_ss, tot_rs, fold_ss, fold_rs, near_ss, near_rs, a_ss, a_rs, b_ss, b_rs):
     me = lax.axis_index("row")
     chips = count // CORES
     chip, core = me // CORES, me % CORES
@@ -108,7 +107,7 @@
     phases, rows, pixels = frames.shape
     half = pixels // 2
     wide = half // CORES
-    drop = wide // 4
+    drop = (wide + 1) // 3
     orders = phases // 2
     mid = phases // 2
     others = [lax.rem(me + step, count) for step in range(1, count)]
@@ -122,6 +121,10 @@
     for p in range(phases):
         frame_loads.append(pltpu.make_async_copy(frames_h.at[0, p], frames.at[p], frame_sem.at[p]))
         frame_loads[p].start()
+    small = []
+    for idx, (source, target) in enumerate(((offset_h, offset), (gain_h, gain), (shift_h, shift))):
+        small.append(pltpu.make_async_copy(source, target, small_sem.at[idx]))
+        small[idx].start()
     loads = []
     for idx, (source, target) in enumerate(
         ((lead_h.at[:, core], lead), (column_h.at[:, chip], column), (inverse_h, inverse), (last_h, last))
@@ -164,6 +167,8 @@
     for load in loads[1:]:
         load.start()
 
+    for load in small:
+        load.wait()
     shift_y, shift_x = shift[0, 0], shift[0, 1]
     inv_cut = 1.0 / (cut_share * pixels)
     scale_out = 0.5 * gain_out / (4.0 * pixels * pixels)
@@ -218,7 +223,7 @@
                     fy = unit_y - offs[j]
                     t = fy * fy + sq_xs[j]
                     r = t * lax.rsqrt(t)
-                    u = jnp.maximum(1.0 - t, 1e-30)
+                    u = jnp.maximum(1.0 - r, 1e-30)
                     v = u * lax.rsqrt(u)
                     acc = poly[0] * r + poly[1]
                     for c in poly[2:]:
@@ -328,11 +333,8 @@
             hi, lo = halves(value)
             spec[0, :, pl.ds((first + k) * wide, wide)] = hi
             spec[1, :, pl.ds((first + k) * wide, wide)] = lo
-        window = pl.ds(first * wide, tiles * wide)
-        mixed[:, window] = dot3(column[0], column[1], spec[0, :, window], spec[1, :, window])
-
-    for load in loads[:2]:
-        load.wait()
+
+    loads[0].wait()
     for k in range(2):
         fold_copy(sib_core, k).wait_recv()
     for order in range(1, orders + 1, 2):
@@ -342,6 +344,10 @@
     for order in range(2, orders + 1, 2):
         spectrum(order - 1)
     spectrum(orders)
+    loads[1].wait()
+    for first, tiles, _ in groups:
+        window = pl.ds(first * wide, tiles * wide)
+        mixed[:, window] = dot3(column[0], column[1], spec[0, :, window], spec[1, :, window])
 
     special = jnp.logical_and(lax.broadcasted_iota(jnp.int32, (STEP, wide), 1) == drop, core == 0)
 
@@ -450,19 +456,21 @@
 
     make_alpha(1)
     combine(1)
-    fourth = rows // 4
-    lane_q = lax.broadcasted_iota(jnp.int32, (fourth, wide), 1)
+    packed = send_b.shape[3]
+    tail_rows = rows - packed
+    lane_t = lax.broadcasted_iota(jnp.int32, (tail_rows, wide), 1)
     for c in far_chips:
         for a in range(2):
             own_rows, far_rows = to_rows(1, a)
             for kc in range(CORES):
                 for k in range(2):
                     piece = far_rows[kc * rows:(kc + 1) * rows, k * wide:(k + 1) * wide]
-                    tail = piece[3 * fourth:]
-                    for i in range(3):
-                        moved = pltpu.roll(tail, wide - drop * (i + 1), 1)
-                        send_b[c, kc, a, pl.ds(i * fourth, fourth), pl.ds(k * wide, wide)] = jnp.where(
-                            lane_q < drop, moved, piece[i * fourth:(i + 1) * fourth])
+                    tail = piece[packed:]
+                    lanes = pl.ds(k * wide, wide)
+                    send_b[c, kc, a, :, lanes] = piece[:packed]
+                    for i, at in enumerate((0, packed - tail_rows)):
+                        send_b[c, kc, a, pl.ds(at, tail_rows), lanes] = jnp.where(
+                            lane_t < drop, pltpu.roll(tail, wide - drop * (i + 1), 1), piece[at:at + tail_rows])
                 b_copy(c, kc, chip, core, a).start()
             keep_near(1, a, own_rows)
 
@@ -487,7 +495,10 @@
     def write_out(a, x, value):
         value = value + part[a, :, pl.ds(x, chunk)]
         for k in range(chunk // 128):
-            woven[x // 128 + k, pl.ds(a, rows, stride=2), :] = value[:, k * 128:(k + 1) * 128]
+            tile = x // 128 + k
+            woven[tile, pl.ds(a, rows, stride=2), :] = value[:, k * 128:(k + 1) * 128]
+            if a:
+                out[:, pl.ds(tile * 128, 128)] = woven[tile]
 
     for a in range(2):
         pieces = []
@@ -503,11 +514,10 @@
         sides = []
         for q in range(2):
             lanes = pl.ds(q * wide, wide)
-            packed = [recv_b[c, k, a, pl.ds(i * fourth, fourth), lanes] for i in range(3)]
-            tail = pltpu.roll(packed[2], 3 * drop, 1)
-            for i in (1, 0):
-                tail = jnp.where(lane_q < (i + 2) * drop, pltpu.roll(packed[i], (i + 1) * drop, 1), tail)
-            sides.append(jnp.concatenate(packed + [tail], axis=0))
+            value = recv_b[c, k, a, :, lanes]
+            first, second = value[:tail_rows], value[packed - tail_rows:]
+            tail = jnp.where(lane_t < 2 * drop, pltpu.roll(first, drop, 1), pltpu.roll(second, 2 * drop, 1))
+            sides.append(jnp.concatenate([value, tail], axis=0))
         return jnp.concatenate(sides, axis=1)
 
     for a in range(2):
@@ -519,8 +529,6 @@
                 value = value + unpacked(c, k, a)
             pieces.append(value)
         finish(a, 1, pieces, write_out)
-    for tile in range(2 * pixels // 128):
-        out[:, pl.ds(tile * 128, 128)] = woven[tile]
 
     for peer in others:
         tot_copy(peer, me).wait_send()
@@ -545,18 +553,22 @@
         half = pixels // 2
         wide = half // CORES
         tiles = 4 * (phases // 2) + 2
+        packed = -(-2 * rows // 24) * 8
+        assert 2 * (rows - packed) <= packed
         lead, column, inverse, last = tables(pixels, count)
         vmem = pl.BlockSpec(memory_space=pltpu.VMEM)
-        smem = pl.BlockSpec(memory_space=pltpu.SMEM)
         hbm = pl.BlockSpec(memory_space=pl.ANY)
         bf16, f32 = jnp.bfloat16, jnp.float32
         dma = pltpu.SemaphoreType.DMA
         return pl.pallas_call(
             functools.partial(kernel, count, otf_polynomial()),
             out_shape=pltpu.VMEM((2 * rows, 2 * pixels), f32),
-            in_specs=[hbm, smem, smem, smem, hbm, hbm, hbm, hbm],
+            in_specs=[hbm] * 8,
             out_specs=vmem,
             scratch_shapes=[
+                pltpu.SMEM(phase_offset.shape, f32),
+                pltpu.SMEM(order_gain.shape, f32),
+                pltpu.SMEM(band_shift.shape, jnp.int32),
                 pltpu.VMEM((phases, rows, pixels), bf16),
                 pltpu.VMEM((2, half, 2 * wide), bf16),
                 pltpu.VMEM((2, pixels, CORES * rows), bf16),
@@ -575,11 +587,11 @@
                 pltpu.VMEM((CORES, 2, 2, rows, 2 * wide), f32),
                 pltpu.VMEM((chips, 2, CORES * rows, 2 * wide), f32),
                 pltpu.VMEM((chips, CORES, 2, rows, 2 * wide), f32),
-                pltpu.VMEM((chips, CORES, 2, 3 * rows // 4, 2 * wide), f32),
-                pltpu.VMEM((chips, CORES, 2, 3 * rows // 4, 2 * wide), f32),
+                pltpu.VMEM((chips, CORES, 2, packed, 2 * wide), f32),
+                pltpu.VMEM((chips, CORES, 2, packed, 2 * wide), f32),
                 pltpu.VMEM((2, rows, 2 * pixels), f32),
                 pltpu.VMEM((2 * pixels // 128, 2 * rows, 128), f32),
-                dma((phases,)), dma((4,)),
+                dma((3,)), dma((phases,)), dma((4,)),
                 dma((count,)), dma((count,)),
                 dma((2,)), dma((2,)),
                 dma((2, 2)), dma((2, 2)),

time: 35.6 us -> 33.8 us (0.949)
  the two profiles are of different devices: /device:TPU:1 before, /device:TPU:0 now
where the time goes in v3:
time: 33.8 us; the launch traced here: 33.3 us
  Pallas kernels  31.6 us (93%)
  local copies, waits for them, and re-layouts  0.97 us (3%)
  between operations  0.66 us (2%)
    pallas_call x1, Pallas kernels, per_device(): pl.pallas_call(functools.partial(kernel, count, otf_polynomial()), out_sh...  31.6 us
    unnamed x1, local copies, waits for them, and re-layouts  0.97 us

profile of v3, /device:TPU:0, one launch (start us, length us, event | category | flops | bytes accessed | tf_op | source)
XLA Modules:
  0.0 33.3 jit_solution(1394071206561041699)
XLA Ops:
  0.7 31.6 %shard_map.82 = f32[256,1024]{1,0:T(8,128)S(1)} custom-call(bf16[1,5,128,512]{3,2,1,0:T(8,128)(2,1)} %frames_h.1, f32[1]{0:T(128)S(6)} %copy.11.offset_h, f32[1,5]{1,0:T(1,128)} %gain_h.1, s32[1,2]{1,0:T(1,128)} %shift_h.1, bf16[2,2,256,256]{3,2,1,0:T(8,128)(2,1)} %constant.8.clone.lead_h, bf16[2,2,512,256]{3,2,1,0:T(8,128)(2,1)} %constant.9.clone.column_h, ...), custom_call_target="tpu_custom_call" | custom-call | tf_op jit(solution)/shard_map/pallas_call | solution.py:563
  32.3 1.0 %copy.10 = f32[256,1024]{1,0:T(8,128)} copy(f32[256,1024]{1,0:T(8,128)S(1)} %shard_map.82) | data formatting | bytes 2097152

commit v4 on v3

--- a/solution.py
+++ b/solution.py
@@ -32,16 +32,20 @@
     return np.cos(angle), np.sin(angle)
 
 
-def lane_order(wide):
-    drop = (wide + 1) // 3
+def limits(pixels, orders):
+    reach = [math.ceil((pixels - cut_share * pixels - k * max_shift(pixels)) / CORES) - 1 for k in (orders - 1, orders)]
+    return reach[0], reach[1]
+
+
+def lane_order(wide, drop):
     return np.concatenate([np.arange(1, drop + 1), [0], np.arange(drop + 1, wide)])
 
 
-def tables(pixels, count):
+def tables(pixels, count, orders):
     half = pixels // 2
     wide = half // CORES
     chips = count // CORES
-    drop = (wide + 1) // 3
+    drop, first = limits(pixels, orders)
     points = np.arange(pixels)
     freqs = np.arange(half)
     alternate = 1.0 - 2.0 * (points % 2)
@@ -60,16 +64,16 @@
     lead, last = [], []
     places = np.arange(pixels)
     for core in range(CORES):
-        own = CORES * lane_order(wide) + core
+        own = CORES * lane_order(wide, drop) + core
         lead.append(np.concatenate([cos_f[:half, own], sin_f[:half, own]], axis=1))
         near_cos, near_sin = cos_sin(places, own, 2 * pixels)
         share = np.where(own == 0, 1.0, 2.0)
         near = np.concatenate([(near_cos * share).T, (-near_sin * share).T])
         mirror = np.where(own == 0, half, pixels - own)
-        assert (pixels - own[:drop]).min() > cut_share * pixels + 2 * max_shift(pixels)
+        assert (pixels - own[:drop]).min() > cut_share * pixels + (orders - 1) * max_shift(pixels)
+        assert (pixels - own[:first]).min() > cut_share * pixels + orders * max_shift(pixels)
         far_cos, far_sin = cos_sin(places, mirror, 2 * pixels)
-        keep = np.where(np.arange(wide) < drop, 0.0, 2.0)
-        far = np.concatenate([(far_cos * keep).T, (-far_sin * keep).T])
+        far = np.concatenate([(far_cos * 2.0).T, (-far_sin * 2.0).T])
         last.append(np.stack([near, far]))
     return tuple(split_table(t) for t in (np.stack(lead), column, inverse, np.stack(last)))
 
@@ -97,9 +101,9 @@
 
 
 def kernel(count, poly, frames_h, offset_h, gain_h, shift_h, lead_h, column_h, inverse_h, last_h, out,
-           offset, gain, shift, frames, lead, column, inverse, last, tot_send, tot, folds, ramps, planes, spec, mixed, alpha, coef,
+           offset, gain, shift, frames, lead, column, inverse, last, tot_send, tot, folds, ramps, planes, spec, mixed, outer, outer_send, outer_recv, mixed_outer, alpha, coef,
            near_send, near, send_a, recv_a, send_b, recv_b, part, woven,
-           small_sem, frame_sem, table_sem, tot_ss, tot_rs, fold_ss, fold_rs, near_ss, near_rs, a_ss, a_rs, b_ss, b_rs):
+           outer_ss, outer_rs, small_sem, frame_sem, table_sem, tot_ss, tot_rs, fold_ss, fold_rs, near_ss, near_rs, a_ss, a_rs, b_ss, b_rs):
     me = lax.axis_index("row")
     chips = count // CORES
     chip, core = me // CORES, me % CORES
@@ -107,8 +111,9 @@
     phases, rows, pixels = frames.shape
     half = pixels // 2
     wide = half // CORES
-    drop = (wide + 1) // 3
     orders = phases // 2
+    drop, first_outer = limits(pixels, orders)
+    turn_outer = drop - first_outer
     mid = phases // 2
     others = [lax.rem(me + step, count) for step in range(1, count)]
     far_chips = [lax.rem(chip + step, chips) for step in range(1, chips)]
@@ -127,7 +132,7 @@
         small[idx].start()
     loads = []
     for idx, (source, target) in enumerate(
-        ((lead_h.at[:, core], lead), (column_h.at[:, chip], column), (inverse_h, inverse), (last_h, last))
+        ((lead_h.at[:, core], lead), (column_h, column), (inverse_h, inverse), (last_h, last))
     ):
         loads.append(pltpu.make_async_copy(source, target, table_sem.at[idx]))
     loads[0].start()
@@ -311,28 +316,45 @@
                         made = [functools.reduce(lambda a, b: a + b, values)]
                     for k, value in enumerate(made):
                         hi, lo = halves(value)
-                        place = (2 * (order - 1) if order else 2 * orders) + k
-                        planes[0, pl.ds(place * span_rows + r, STEP), lanes_at] = hi
-                        planes[1, pl.ds(place * span_rows + r, STEP), lanes_at] = lo
+                        place = 2 * (order - 1) * span_rows + 2 * r + k * STEP if order else 2 * orders * span_rows + r
+                        planes[0, pl.ds(place, STEP), lanes_at] = hi
+                        planes[1, pl.ds(place, STEP), lanes_at] = lo
+
+    forward = shift_x >= 0
+
+    def outer_copy(c, slot_chip):
+        return pltpu.make_async_remote_copy(
+            src_ref=outer_send, dst_ref=outer_recv.at[slot_chip],
+            send_sem=outer_ss.at[c], recv_sem=outer_rs.at[slot_chip],
+            device_id={"row": c * CORES + core}, device_id_type=MESH)
 
     def spectrum(g):
         first, tiles, order = groups[g]
         place = 2 * (order - 1) if order else 2 * orders
         span = pl.ds(place * span_rows, (2 if order else 1) * span_rows)
         result = dot3(planes[0, span, :], planes[1, span, :], lead[0], lead[1])
-        special = jnp.logical_and(
-            lax.broadcasted_iota(jnp.int32, (span_rows, wide), 1) == drop, core == 0)
-        if order:
-            cr, sr = result[:span_rows, :wide], result[:span_rows, wide:]
-            ci, si = result[span_rows:, :wide], result[span_rows:, wide:]
-            values = [jnp.where(special, cr, cr + si), jnp.where(special, ci, ci - sr),
-                      jnp.where(special, sr, cr - si), jnp.where(special, si, ci + sr)]
-        else:
-            values = [result[:, :wide], jnp.where(special, 0.0, -result[:, wide:])]
-        for k, value in enumerate(values):
-            hi, lo = halves(value)
-            spec[0, :, pl.ds((first + k) * wide, wide)] = hi
-            spec[1, :, pl.ds((first + k) * wide, wide)] = lo
+        special = jnp.logical_and(lax.broadcasted_iota(jnp.int32, (STEP, wide), 1) == drop, core == 0)
+        for r in range(0, span_rows, STEP):
+            if order:
+                re, im = result[2 * r:2 * r + STEP], result[2 * r + STEP:2 * r + 2 * STEP]
+                cr, sr, ci, si = re[:, :wide], re[:, wide:], im[:, :wide], im[:, wide:]
+                values = [jnp.where(special, cr, cr + si), jnp.where(special, ci, ci - sr),
+                          jnp.where(special, sr, cr - si), jnp.where(special, si, ci + sr)]
+            else:
+                re = result[r:r + STEP]
+                values = [re[:, :wide], jnp.where(special, 0.0, -re[:, wide:])]
+            for k, value in enumerate(values):
+                hi, lo = halves(value)
+                spec[0, pl.ds(r, STEP), pl.ds((first + k) * wide, wide)] = hi
+                spec[1, pl.ds(r, STEP), pl.ds((first + k) * wide, wide)] = lo
+            if order == orders:
+                outer_re = jnp.where(forward, values[2], values[0])
+                outer_im = jnp.where(forward, values[3], -values[1])
+                outer[pl.ds(r, STEP), pl.ds(0, wide)] = outer_re
+                outer[pl.ds(r, STEP), pl.ds(wide, wide)] = outer_im
+                lane = lax.broadcasted_iota(jnp.int32, (STEP, wide), 1)
+                here = jnp.logical_and(lane >= first_outer, lane < drop)
+                outer_send[pl.ds(r, STEP), :] = jnp.where(here, outer_re, pltpu.roll(outer_im, turn_outer, 1))
 
     loads[0].wait()
     for k in range(2):
@@ -343,13 +365,17 @@
     unmix(list(range(2, orders + 1, 2)) + [0])
     for order in range(2, orders + 1, 2):
         spectrum(order - 1)
+    for c in far_chips:
+        outer_copy(c, chip).start()
     spectrum(orders)
     loads[1].wait()
     for first, tiles, _ in groups:
         window = pl.ds(first * wide, tiles * wide)
-        mixed[:, window] = dot3(column[0], column[1], spec[0, :, window], spec[1, :, window])
+        mixed[:, window] = dot3(column[0, chip], column[1, chip], spec[0, :, window], spec[1, :, window])
 
     special = jnp.logical_and(lax.broadcasted_iota(jnp.int32, (STEP, wide), 1) == drop, core == 0)
+
+    outer_lanes = lax.broadcasted_iota(jnp.int32, (STEP, wide), 1) < drop
 
     def combine(side):
         def block(first, odd, second, top):
@@ -362,9 +388,9 @@
             def pick(at_top, value):
                 return jnp.where(row0, at_top, value) if top else value
 
-            def signs(tile):
+            def signs(tile, source=mixed):
                 re, im = pl.ds(tile * wide, wide), pl.ds((tile + 1) * wide, wide)
-                cr, ci, sr, si = mixed[here, re], mixed[here, im], mixed[below, re], mixed[below, im]
+                cr, ci, sr, si = source[here, re], source[here, im], source[below, re], source[below, im]
                 plus = (pick(cr, cr + si), pick(ci, ci - sr))
                 minus = (pick(sr, cr - si), pick(si, ci + sr))
                 return plus, minus
@@ -394,6 +420,12 @@
                     up, down = alpha[side, slot, mid + order, here, :], alpha[side, slot, mid - order, here, :]
                     add(slot, 0, up * direct[s][0] + down * swap[s][0])
                     add(slot, 1, up * direct[s][1] - down * swap[s][1])
+            if side:
+                single_order = signs(0, mixed_outer)
+                for slot in slots:
+                    weight = jnp.where(forward, alpha[side, slot, mid + orders, here, :], alpha[side, slot, mid - orders, here, :])
+                    for k in range(2):
+                        sums[slot][k] = jnp.where(outer_lanes, weight * single_order[slot % 2][k], sums[slot][k])
             for a in range(2):
                 def folded(s, k):
                     if not second:
@@ -428,7 +460,7 @@
 
     def a_copy(c, kc, slot_chip, slot_core, a):
         return pltpu.make_async_remote_copy(
-            src_ref=send_a.at[c, a, pl.ds(kc * rows, rows), :], dst_ref=recv_a.at[slot_chip, slot_core, a],
+            src_ref=send_a.at[c, a, pl.ds(pl.multiple_of(kc * rows, rows), rows), :], dst_ref=recv_a.at[slot_chip, slot_core, a],
             send_sem=a_ss.at[c, kc, a], recv_sem=a_rs.at[slot_chip, slot_core, a],
             device_id={"row": c * CORES + kc}, device_id_type=MESH)
 
@@ -450,27 +482,38 @@
         for a in range(2):
             own_rows, far_rows = to_rows(0, a)
             send_a[c, a] = far_rows
-            for kc in range(CORES):
+            for kc in (core, sib_core):
                 a_copy(c, kc, chip, core, a).start()
             keep_near(0, a, own_rows)
 
     make_alpha(1)
+    hi, lo = halves(outer[...])
+    mixed_outer[...] = dot3(column[0, chip], column[1, chip], hi, lo)
+    for c in far_chips:
+        outer_copy(c, c).wait_recv()
+        re = outer_recv[c]
+        hi, lo = halves(jnp.concatenate([re, pltpu.roll(re, wide - turn_outer, 1)], axis=1))
+        mixed_outer[...] += dot3(column[0, c], column[1, c], hi, lo)
     combine(1)
     packed = send_b.shape[3]
-    tail_rows = rows - packed
+    tail_rows = (rows - packed) // 2
+    kept = wide - drop
     lane_t = lax.broadcasted_iota(jnp.int32, (tail_rows, wide), 1)
+    kept_lanes = lax.broadcasted_iota(jnp.int32, (rows, wide), 1) >= drop
     for c in far_chips:
         for a in range(2):
             own_rows, far_rows = to_rows(1, a)
             for kc in range(CORES):
                 for k in range(2):
                     piece = far_rows[kc * rows:(kc + 1) * rows, k * wide:(k + 1) * wide]
-                    tail = piece[packed:]
                     lanes = pl.ds(k * wide, wide)
+                    second, third = piece[packed:packed + tail_rows], piece[packed + tail_rows:]
                     send_b[c, kc, a, :, lanes] = piece[:packed]
-                    for i, at in enumerate((0, packed - tail_rows)):
-                        send_b[c, kc, a, pl.ds(at, tail_rows), lanes] = jnp.where(
-                            lane_t < drop, pltpu.roll(tail, wide - drop * (i + 1), 1), piece[at:at + tail_rows])
+                    send_b[c, kc, a, pl.ds(0, tail_rows), lanes] = jnp.where(
+                        lane_t >= drop, piece[:tail_rows],
+                        jnp.where(lane_t >= drop - kept, pltpu.roll(second, wide - kept, 1),
+                                  pltpu.roll(third, wide - 2 * kept, 1)))
+            for kc in (core, sib_core):
                 b_copy(c, kc, chip, core, a).start()
             keep_near(1, a, own_rows)
 
@@ -491,14 +534,6 @@
 
     def write_part(a, x, value):
         part[a, :, pl.ds(x, chunk)] = value
-
-    def write_out(a, x, value):
-        value = value + part[a, :, pl.ds(x, chunk)]
-        for k in range(chunk // 128):
-            tile = x // 128 + k
-            woven[tile, pl.ds(a, rows, stride=2), :] = value[:, k * 128:(k + 1) * 128]
-            if a:
-                out[:, pl.ds(tile * 128, 128)] = woven[tile]
 
     for a in range(2):
         pieces = []
@@ -515,25 +550,39 @@
         for q in range(2):
             lanes = pl.ds(q * wide, wide)
             value = recv_b[c, k, a, :, lanes]
-            first, second = value[:tail_rows], value[packed - tail_rows:]
-            tail = jnp.where(lane_t < 2 * drop, pltpu.roll(first, drop, 1), pltpu.roll(second, 2 * drop, 1))
-            sides.append(jnp.concatenate([value, tail], axis=0))
+            first = value[:tail_rows]
+            joined = jnp.concatenate([value, pltpu.roll(first, kept, 1), pltpu.roll(first, 2 * kept, 1)], axis=0)
+            sides.append(jnp.where(kept_lanes, joined, 0.0))
         return jnp.concatenate(sides, axis=1)
 
     for a in range(2):
-        pieces = []
-        for k in range(CORES):
+        for k in (core, sib_core):
+            sign = jnp.where(k == 0, 1.0, -1.0)
             value = near[k, 1, a]
             for c in far_chips:
                 b_copy(c, k, c, k, a).wait_recv()
                 value = value + unpacked(c, k, a)
-            pieces.append(value)
-        finish(a, 1, pieces, write_out)
+            hi, lo = halves(value)
+            for x in range(0, pixels, chunk):
+                span = pl.ds(x, chunk)
+                value = dot3(hi, lo, last[0, k, 1, :, span], last[1, k, 1, :, span])
+                for at, term in ((x, value), (pixels + x, sign * value)):
+                    total = part[a, :, pl.ds(at, chunk)] + term
+                    if k is core:
+                        part[a, :, pl.ds(at, chunk)] = total
+                        continue
+                    for q in range(chunk // 128):
+                        tile = at // 128 + q
+                        woven[tile, pl.ds(a, rows, stride=2), :] = total[:, q * 128:(q + 1) * 128]
+                        if a:
+                            out[:, pl.ds(tile * 128, 128)] = woven[tile]
 
     for peer in others:
         tot_copy(peer, me).wait_send()
     for k in range(2):
         fold_copy(core, k).wait_send()
+    for c in far_chips:
+        outer_copy(c, chip).wait_send()
     for a in range(2):
         for side in range(2):
             near_copy(core, side, a).wait_send()
@@ -553,9 +602,11 @@
         half = pixels // 2
         wide = half // CORES
         tiles = 4 * (phases // 2) + 2
-        packed = -(-2 * rows // 24) * 8
-        assert 2 * (rows - packed) <= packed
-        lead, column, inverse, last = tables(pixels, count)
+        packed = -(-rows // 24) * 8
+        orders = phases // 2
+        drop, first_outer = limits(pixels, orders)
+        assert rows - packed <= 2 * packed and 3 * (wide - drop) <= wide and 2 * (drop - first_outer) <= wide
+        lead, column, inverse, last = tables(pixels, count, orders)
         vmem = pl.BlockSpec(memory_space=pltpu.VMEM)
         hbm = pl.BlockSpec(memory_space=pl.ANY)
         bf16, f32 = jnp.bfloat16, jnp.float32
@@ -571,7 +622,7 @@
                 pltpu.SMEM(band_shift.shape, jnp.int32),
                 pltpu.VMEM((phases, rows, pixels), bf16),
                 pltpu.VMEM((2, half, 2 * wide), bf16),
-                pltpu.VMEM((2, pixels, CORES * rows), bf16),
+                pltpu.VMEM(column.shape, bf16),
                 pltpu.VMEM(inverse.shape, bf16),
                 pltpu.VMEM(last.shape, bf16),
                 pltpu.VMEM((8, 128), f32),
@@ -581,6 +632,10 @@
                 pltpu.VMEM((2, phases * CORES * rows, half), bf16),
                 pltpu.VMEM((2, CORES * rows, tiles * wide), bf16),
                 pltpu.VMEM((pixels, tiles * wide), f32),
+                pltpu.VMEM((CORES * rows, 2 * wide), f32),
+                pltpu.VMEM((CORES * rows, wide), f32),
+                pltpu.VMEM((chips, CORES * rows, wide), f32),
+                pltpu.VMEM((pixels, 2 * wide), f32),
                 pltpu.VMEM((2, 4, phases, half, wide), f32),
                 pltpu.VMEM((2, 2, 2, 2, half, 2 * wide), bf16),
                 pltpu.VMEM((2, 2, rows, 2 * wide), f32),
@@ -591,6 +646,7 @@
                 pltpu.VMEM((chips, CORES, 2, packed, 2 * wide), f32),
                 pltpu.VMEM((2, rows, 2 * pixels), f32),
                 pltpu.VMEM((2 * pixels // 128, 2 * rows, 128), f32),
+                dma((chips,)), dma((chips,)),
                 dma((3,)), dma((phases,)), dma((4,)),
                 dma((count,)), dma((count,)),
                 dma((2,)), dma((2,)),

time: 33.8 us -> 31 us (0.917); the launches traced: 33.3 us -> 30.8 us
  Pallas kernels: 31.6 us -> 29.2 us
    pallas_call x1, Pallas kernels: 31.6 us -> 29.2 us  [per_device(): pl.pallas_call(functools.partial(kernel, count, otf_polynomial()), out_sh...]
where the time goes in v4:
time: 31 us; the launch traced here: 30.8 us
  Pallas kernels  29.2 us (94%)
  local copies, waits for them, and re-layouts  0.97 us (3%)
  between operations  0.66 us (2%)
    pallas_call x1, Pallas kernels, per_device(): pl.pallas_call(functools.partial(kernel, count, otf_polynomial()), out_sh...  29.2 us
    unnamed x1, local copies, waits for them, and re-layouts  0.97 us

profile of v4, /device:TPU:0, one launch (start us, length us, event | category | flops | bytes accessed | tf_op | source)
XLA Modules:
  0.0 30.8 jit_solution(5689337108545224093)
XLA Ops:
  0.7 29.2 %shard_map.82 = f32[256,1024]{1,0:T(8,128)S(1)} custom-call(bf16[1,5,128,512]{3,2,1,0:T(8,128)(2,1)} %frames_h.1, f32[1]{0:T(128)S(6)} %copy.11.offset_h, f32[1,5]{1,0:T(1,128)} %gain_h.1, s32[1,2]{1,0:T(1,128)} %shift_h.1, bf16[2,2,256,256]{3,2,1,0:T(8,128)(2,1)} %constant.8.clone.lead_h, bf16[2,2,512,256]{3,2,1,0:T(8,128)(2,1)} %constant.9.clone.column_h, ...), custom_call_target="tpu_custom_call" | custom-call | tf_op jit(solution)/shard_map/pallas_call | solution.py:614
  29.9 1.0 %copy.10 = f32[256,1024]{1,0:T(8,128)} copy(f32[256,1024]{1,0:T(8,128)S(1)} %shard_map.82) | data formatting | bytes 2097152

commit v5 on v4

--- a/solution.py
+++ b/solution.py
@@ -33,8 +33,10 @@
 
 
 def limits(pixels, orders):
-    reach = [math.ceil((pixels - cut_share * pixels - k * max_shift(pixels)) / CORES) - 1 for k in (orders - 1, orders)]
-    return reach[0], reach[1]
+    lone, first = [math.ceil((pixels - cut_share * pixels - k * max_shift(pixels)) / CORES) - 1
+                   for k in (orders - 1, orders)]
+    wide = pixels // 2 // CORES
+    return max(lone, wide - wide // 4), lone, first
 
 
 def lane_order(wide, drop):
@@ -45,7 +47,7 @@
     half = pixels // 2
     wide = half // CORES
     chips = count // CORES
-    drop, first = limits(pixels, orders)
+    drop, lone, first = limits(pixels, orders)
     points = np.arange(pixels)
     freqs = np.arange(half)
     alternate = 1.0 - 2.0 * (points % 2)
@@ -70,7 +72,7 @@
         share = np.where(own == 0, 1.0, 2.0)
         near = np.concatenate([(near_cos * share).T, (-near_sin * share).T])
         mirror = np.where(own == 0, half, pixels - own)
-        assert (pixels - own[:drop]).min() > cut_share * pixels + (orders - 1) * max_shift(pixels)
+        assert (pixels - own[:lone]).min() > cut_share * pixels + (orders - 1) * max_shift(pixels)
         assert (pixels - own[:first]).min() > cut_share * pixels + orders * max_shift(pixels)
         far_cos, far_sin = cos_sin(places, mirror, 2 * pixels)
         far = np.concatenate([(far_cos * 2.0).T, (-far_sin * 2.0).T])
@@ -112,8 +114,8 @@
     half = pixels // 2
     wide = half // CORES
     orders = phases // 2
-    drop, first_outer = limits(pixels, orders)
-    turn_outer = drop - first_outer
+    drop, lone, first_outer = limits(pixels, orders)
+    turn_outer, pair = drop - first_outer, drop - lone
     mid = phases // 2
     others = [lax.rem(me + step, count) for step in range(1, count)]
     far_chips = [lax.rem(chip + step, chips) for step in range(1, chips)]
@@ -321,6 +323,7 @@
                         planes[1, pl.ds(place, STEP), lanes_at] = lo
 
     forward = shift_x >= 0
+    free = first_outer + 2 * turn_outer - wide
 
     def outer_copy(c, slot_chip):
         return pltpu.make_async_remote_copy(
@@ -347,14 +350,22 @@
                 hi, lo = halves(value)
                 spec[0, pl.ds(r, STEP), pl.ds((first + k) * wide, wide)] = hi
                 spec[1, pl.ds(r, STEP), pl.ds((first + k) * wide, wide)] = lo
-            if order == orders:
+            if order >= orders - 1:
+                place = (orders - order) * 2 * wide
                 outer_re = jnp.where(forward, values[2], values[0])
                 outer_im = jnp.where(forward, values[3], -values[1])
-                outer[pl.ds(r, STEP), pl.ds(0, wide)] = outer_re
-                outer[pl.ds(r, STEP), pl.ds(wide, wide)] = outer_im
+                outer[pl.ds(r, STEP), pl.ds(place, wide)] = outer_re
+                outer[pl.ds(r, STEP), pl.ds(place + wide, wide)] = outer_im
                 lane = lax.broadcasted_iota(jnp.int32, (STEP, wide), 1)
-                here = jnp.logical_and(lane >= first_outer, lane < drop)
-                outer_send[pl.ds(r, STEP), :] = jnp.where(here, outer_re, pltpu.roll(outer_im, turn_outer, 1))
+                if order == orders:
+                    here = jnp.logical_and(lane >= first_outer, lane < drop)
+                    full = jnp.where(here, outer_re, pltpu.roll(outer_im, turn_outer, 1))
+                    below = jnp.logical_and(lane >= free, lane < free + 2 * pair)
+                    outer_send[pl.ds(r, STEP), :] = jnp.where(below, outer_send[pl.ds(r, STEP), :], full)
+                else:
+                    outer_send[pl.ds(r, STEP), :] = jnp.where(
+                        lane < free + pair, pltpu.roll(outer_re, wide - (lone - free), 1),
+                        pltpu.roll(outer_im, wide - (lone - free - pair), 1))
 
     loads[0].wait()
     for k in range(2):
@@ -421,11 +432,13 @@
                     add(slot, 0, up * direct[s][0] + down * swap[s][0])
                     add(slot, 1, up * direct[s][1] - down * swap[s][1])
             if side:
-                single_order = signs(0, mixed_outer)
+                outer_parts = [(orders - q, signs(2 * q, mixed_outer)) for q in range(2)]
                 for slot in slots:
-                    weight = jnp.where(forward, alpha[side, slot, mid + orders, here, :], alpha[side, slot, mid - orders, here, :])
+                    weights = [jnp.where(forward, alpha[side, slot, mid + order, here, :],
+                                         alpha[side, slot, mid - order, here, :]) for order, _ in outer_parts]
                     for k in range(2):
-                        sums[slot][k] = jnp.where(outer_lanes, weight * single_order[slot % 2][k], sums[slot][k])
+                        whole = weights[0] * outer_parts[0][1][slot % 2][k] + weights[1] * outer_parts[1][1][slot % 2][k]
+                        sums[slot][k] = jnp.where(outer_lanes, whole, sums[slot][k])
             for a in range(2):
                 def folded(s, k):
                     if not second:
@@ -491,14 +504,15 @@
     mixed_outer[...] = dot3(column[0, chip], column[1, chip], hi, lo)
     for c in far_chips:
         outer_copy(c, c).wait_recv()
-        re = outer_recv[c]
-        hi, lo = halves(jnp.concatenate([re, pltpu.roll(re, wide - turn_outer, 1)], axis=1))
+        tile = outer_recv[c]
+        hi, lo = halves(jnp.concatenate([tile, pltpu.roll(tile, wide - turn_outer, 1), pltpu.roll(tile, lone - free, 1),
+                                         pltpu.roll(tile, lone - free - pair, 1)], axis=1))
         mixed_outer[...] += dot3(column[0, c], column[1, c], hi, lo)
     combine(1)
     packed = send_b.shape[3]
-    tail_rows = (rows - packed) // 2
+    shared = rows // packed
     kept = wide - drop
-    lane_t = lax.broadcasted_iota(jnp.int32, (tail_rows, wide), 1)
+    lane_t = lax.broadcasted_iota(jnp.int32, (packed, wide), 1)
     kept_lanes = lax.broadcasted_iota(jnp.int32, (rows, wide), 1) >= drop
     for c in far_chips:
         for a in range(2):
@@ -507,12 +521,11 @@
                 for k in range(2):
                     piece = far_rows[kc * rows:(kc + 1) * rows, k * wide:(k + 1) * wide]
                     lanes = pl.ds(k * wide, wide)
-                    second, third = piece[packed:packed + tail_rows], piece[packed + tail_rows:]
-                    send_b[c, kc, a, :, lanes] = piece[:packed]
-                    send_b[c, kc, a, pl.ds(0, tail_rows), lanes] = jnp.where(
-                        lane_t >= drop, piece[:tail_rows],
-                        jnp.where(lane_t >= drop - kept, pltpu.roll(second, wide - kept, 1),
-                                  pltpu.roll(third, wide - 2 * kept, 1)))
+                    value = piece[:packed]
+                    for i in range(1, shared):
+                        moved = pltpu.roll(piece[i * packed:(i + 1) * packed], wide - i * kept, 1)
+                        value = jnp.where(lane_t < wide - i * kept, moved, value)
+                    send_b[c, kc, a, :, lanes] = value
             for kc in (core, sib_core):
                 b_copy(c, kc, chip, core, a).start()
             keep_near(1, a, own_rows)
@@ -550,8 +563,7 @@
         for q in range(2):
             lanes = pl.ds(q * wide, wide)
             value = recv_b[c, k, a, :, lanes]
-            first = value[:tail_rows]
-            joined = jnp.concatenate([value, pltpu.roll(first, kept, 1), pltpu.roll(first, 2 * kept, 1)], axis=0)
+            joined = jnp.concatenate([value] + [pltpu.roll(value, i * kept, 1) for i in range(1, shared)], axis=0)
             sides.append(jnp.where(kept_lanes, joined, 0.0))
         return jnp.concatenate(sides, axis=1)
 
@@ -602,10 +614,10 @@
         half = pixels // 2
         wide = half // CORES
         tiles = 4 * (phases // 2) + 2
-        packed = -(-rows // 24) * 8
+        packed = rows // 4
         orders = phases // 2
-        drop, first_outer = limits(pixels, orders)
-        assert rows - packed <= 2 * packed and 3 * (wide - drop) <= wide and 2 * (drop - first_outer) <= wide
+        drop, lone, first = limits(pixels, orders)
+        assert 4 * (wide - drop) <= wide and 2 * (drop - first) + 2 * (drop - lone) <= wide < 2 * drop
         lead, column, inverse, last = tables(pixels, count, orders)
         vmem = pl.BlockSpec(memory_space=pltpu.VMEM)
         hbm = pl.BlockSpec(memory_space=pl.ANY)
@@ -632,10 +644,10 @@
                 pltpu.VMEM((2, phases * CORES * rows, half), bf16),
                 pltpu.VMEM((2, CORES * rows, tiles * wide), bf16),
                 pltpu.VMEM((pixels, tiles * wide), f32),
-                pltpu.VMEM((CORES * rows, 2 * wide), f32),
+                pltpu.VMEM((CORES * rows, 4 * wide), f32),
                 pltpu.VMEM((CORES * rows, wide), f32),
                 pltpu.VMEM((chips, CORES * rows, wide), f32),
-                pltpu.VMEM((pixels, 2 * wide), f32),
+                pltpu.VMEM((pixels, 4 * wide), f32),
                 pltpu.VMEM((2, 4, phases, half, wide), f32),
                 pltpu.VMEM((2, 2, 2, 2, half, 2 * wide), bf16),
                 pltpu.VMEM((2, 2, rows, 2 * wide), f32),

time: 31 us -> 29.8 us (0.961)
  Pallas kernels: 29.2 us -> 28 us
    pallas_call x1, Pallas kernels: 29.2 us -> 28 us  [per_device(): pl.pallas_call(functools.partial(kernel, count, otf_polynomial()), out_sh...]
where the time goes in v5:
time: 29.8 us; the launch traced here: 29.7 us
  Pallas kernels  28 us (94%)
  local copies, waits for them, and re-layouts  0.97 us (3%)
  between operations  0.66 us (2%)
    pallas_call x1, Pallas kernels, per_device(): pl.pallas_call(functools.partial(kernel, count, otf_polynomial()), out_sh...  28 us
    unnamed x1, local copies, waits for them, and re-layouts  0.97 us

profile of v5, /device:TPU:0, one launch (start us, length us, event | category | flops | bytes accessed | tf_op | source)
XLA Modules:
  0.0 29.7 jit_solution(2285560447605038183)
XLA Ops:
  0.7 28.0 %shard_map.82 = f32[256,1024]{1,0:T(8,128)S(1)} custom-call(bf16[1,5,128,512]{3,2,1,0:T(8,128)(2,1)} %frames_h.1, f32[1]{0:T(128)S(6)} %copy.11.offset_h, f32[1,5]{1,0:T(1,128)} %gain_h.1, s32[1,2]{1,0:T(1,128)} %shift_h.1, bf16[2,2,256,256]{3,2,1,0:T(8,128)(2,1)} %constant.8.clone.lead_h, bf16[2,2,512,256]{3,2,1,0:T(8,128)(2,1)} %constant.9.clone.column_h, ...), custom_call_target="tpu_custom_call" | custom-call | tf_op jit(solution)/shard_map/pallas_call | solution.py:626
  28.7 1.0 %copy.10 = f32[256,1024]{1,0:T(8,128)} copy(f32[256,1024]{1,0:T(8,128)S(1)} %shard_map.82) | data formatting | bytes 2097152

commit v6 on v5

--- a/solution.py
+++ b/solution.py
@@ -103,7 +103,7 @@
 
 
 def kernel(count, poly, frames_h, offset_h, gain_h, shift_h, lead_h, column_h, inverse_h, last_h, out,
-           offset, gain, shift, frames, lead, column, inverse, last, tot_send, tot, folds, ramps, planes, spec, mixed, outer, outer_send, outer_recv, mixed_outer, alpha, coef,
+           offset, gain, shift, frames, lead, column, inverse, last, tot_send, tot, folds, ramps, planes, spec, mixed, outer_send, outer_recv, mixed_outer, alpha, coef,
            near_send, near, send_a, recv_a, send_b, recv_b, part, woven,
            outer_ss, outer_rs, small_sem, frame_sem, table_sem, tot_ss, tot_rs, fold_ss, fold_rs, near_ss, near_rs, a_ss, a_rs, b_ss, b_rs):
     me = lax.axis_index("row")
@@ -351,11 +351,8 @@
                 spec[0, pl.ds(r, STEP), pl.ds((first + k) * wide, wide)] = hi
                 spec[1, pl.ds(r, STEP), pl.ds((first + k) * wide, wide)] = lo
             if order >= orders - 1:
-                place = (orders - order) * 2 * wide
                 outer_re = jnp.where(forward, values[2], values[0])
                 outer_im = jnp.where(forward, values[3], -values[1])
-                outer[pl.ds(r, STEP), pl.ds(place, wide)] = outer_re
-                outer[pl.ds(r, STEP), pl.ds(place + wide, wide)] = outer_im
                 lane = lax.broadcasted_iota(jnp.int32, (STEP, wide), 1)
                 if order == orders:
                     here = jnp.logical_and(lane >= first_outer, lane < drop)
@@ -500,7 +497,14 @@
             keep_near(0, a, own_rows)
 
     make_alpha(1)
-    hi, lo = halves(outer[...])
+    own = [[], []]
+    for order in (orders, orders - 1):
+        tiles = [pl.ds((4 * (order - 1) + k) * wide, wide) for k in range(4)]
+        for part_at in range(2):
+            plus_re, plus_im, minus_re, minus_im = [spec[part_at, :, t].astype(jnp.float32) for t in tiles]
+            own[part_at].append(jnp.where(forward, minus_re, plus_re).astype(jnp.bfloat16))
+            own[part_at].append(jnp.where(forward, minus_im, -plus_im).astype(jnp.bfloat16))
+    hi, lo = [jnp.concatenate(value, axis=1) for value in own]
     mixed_outer[...] = dot3(column[0, chip], column[1, chip], hi, lo)
     for c in far_chips:
         outer_copy(c, c).wait_recv()
@@ -644,7 +648,6 @@
                 pltpu.VMEM((2, phases * CORES * rows, half), bf16),
                 pltpu.VMEM((2, CORES * rows, tiles * wide), bf16),
                 pltpu.VMEM((pixels, tiles * wide), f32),
-                pltpu.VMEM((CORES * rows, 4 * wide), f32),
                 pltpu.VMEM((CORES * rows, wide), f32),
                 pltpu.VMEM((chips, CORES * rows, wide), f32),
                 pltpu.VMEM((pixels, 4 * wide), f32),

time: 29.8 us -> 29.8 us (level)
  no operation moved by 1% of the time
where the time goes in v6:
time: 29.8 us; the launch traced here: 29.6 us
  Pallas kernels  28 us (94%)
  local copies, waits for them, and re-layouts  0.97 us (3%)
  between operations  0.66 us (2%)
    pallas_call x1, Pallas kernels, per_device(): pl.pallas_call(functools.partial(kernel, count, otf_polynomial()), out_sh...  28 us
    unnamed x1, local copies, waits for them, and re-layouts  0.97 us

profile of v6, /device:TPU:0, one launch (start us, length us, event | category | flops | bytes accessed | tf_op | source)
XLA Modules:
  0.0 29.6 jit_solution(2995165379163877849)
XLA Ops:
  0.7 28.0 %shard_map.82 = f32[256,1024]{1,0:T(8,128)S(1)} custom-call(bf16[1,5,128,512]{3,2,1,0:T(8,128)(2,1)} %frames_h.1, f32[1]{0:T(128)S(6)} %copy.11.offset_h, f32[1,5]{1,0:T(1,128)} %gain_h.1, s32[1,2]{1,0:T(1,128)} %shift_h.1, bf16[2,2,256,256]{3,2,1,0:T(8,128)(2,1)} %constant.8.clone.lead_h, bf16[2,2,512,256]{3,2,1,0:T(8,128)(2,1)} %constant.9.clone.column_h, ...), custom_call_target="tpu_custom_call" | custom-call | tf_op jit(solution)/shard_map/pallas_call | solution.py:630
  28.7 1.0 %copy.10 = f32[256,1024]{1,0:T(8,128)} copy(f32[256,1024]{1,0:T(8,128)S(1)} %shard_map.82) | data formatting | bytes 2097152
